TPU v7x, 32 devices: a whole 2x2x4 slice. The times are simulated.
32 devices in a mesh: section: 2 (over y), dp: 16 (over z, x, core).
Axes of the slice: x: 2, y: 2, z: 4, core: 2. Of those that a mesh axis runs over, the one named last changes fastest.
Arguments:
- inputs: bfloat16 [4, 16, 198, 768], P(None, 'dp'), may hold values from -6 to 6
- ln1_gain: float32 [2, 768], P('section'), may hold values from 0.1 to 1.9
- ln1_bias: float32 [2, 768], P('section'), may hold values from -3 to 3
- qkv_weight: bfloat16 [2, 768, 2304], P('section'), may hold values from -0.21875 to 0.21875
- qv_bias: float32 [2, 1536], P('section'), may hold values from -3 to 3
- proj_weight: bfloat16 [2, 768, 768], P('section'), may hold values from -0.625 to 0.625
- proj_bias: float32 [2, 768], P('section'), may hold values from -3 to 3
- ln2_gain: float32 [2, 768], P('section'), may hold values from 0.1 to 1.9
- ln2_bias: float32 [2, 768], P('section'), may hold values from -3 to 3
- fc1_weight: bfloat16 [2, 768, 3072], P('section'), may hold values from -0.21875 to 0.21875
- fc1_bias: float32 [2, 3072], P('section'), may hold values from -3 to 3
- fc2_weight: bfloat16 [2, 3072, 768], P('section'), may hold values from -0.15625 to 0.15625
- fc2_bias: float32 [2, 768], P('section'), may hold values from -3 to 3
- keep_masks: int32 [2, 2, 4, 16], P('section', None, None, 'dp'), may hold values 0 or 1
- cotangent: bfloat16 [4, 16, 198, 768], P(None, 'dp'), may hold values from -6 to 6
Outputs:
- layer_outputs: bfloat16 [2, 4, 16, 198, 768], P('section', None, 'dp')
- input_grads: bfloat16 [2, 4, 16, 198, 768], P('section', None, 'dp')
- grad_ln1_gain: float32 [2, 768], P('section')
- grad_ln1_bias: float32 [2, 768], P('section')
- grad_qkv_weight: float32 [2, 768, 2304], P('section')
- grad_qv_bias: float32 [2, 1536], P('section')
- grad_proj_weight: float32 [2, 768, 768], P('section')
- grad_proj_bias: float32 [2, 768], P('section')
- grad_ln2_gain: float32 [2, 768], P('section')
- grad_ln2_bias: float32 [2, 768], P('section')
- grad_fc1_weight: float32 [2, 768, 3072], P('section')
- grad_fc1_bias: float32 [2, 3072], P('section')
- grad_fc2_weight: float32 [2, 3072, 768], P('section')
- grad_fc2_bias: float32 [2, 768], P('section')
Inputs may be any that keep to these rules, and one draw needn't show every extreme that they name: `keep_masks`: 1 keeps a branch for that image, 0 drops it.
All inputs are finite; a program needn't handle non-finite values. No bound on the sum of `keep_masks` on one device may be relied on, other than what follows from the above.
Results may differ from a plain program's by a relative error of at most 0.015.
Values may be sent and summed in bfloat16 or wider, within the bound.
A program may use at most 256 MiB of HBM per device.

v0:
```python
import math

import jax
import jax.numpy as jnp
from jax import lax
from jax.sharding import PartitionSpec as P

HEAD_DIM = 64


epsilon = 1e-06
survive = 1.0 / 0.9


def from_behind(value, axis, steps):
    count = lax.axis_size(axis)
    initial, last = (max(0, -steps), min(count, count - steps))
    return lax.ppermute(value, axis, [(source, source + steps) for source in range(initial, last)])


def as_sent(x):

    def short(part):
        return part.astype(jnp.bfloat16) if part.dtype == jnp.float32 else part

    return jax.tree.map(short, x)


def norm_parts(values, gain, shift):
    mean_v = jnp.mean(values, axis=-1, keepdims=True)
    centered = values - mean_v
    var = jnp.mean(centered * centered, axis=-1, keepdims=True)
    factor = lax.rsqrt(var + epsilon)
    normed = centered * factor
    return (normed * gain + shift, normed, factor)


def norm_back(grad_out, normed, factor, gain):
    scaled = grad_out * gain
    grad_in = factor * (
        scaled
        - jnp.mean(scaled, axis=-1, keepdims=True)
        - normed * jnp.mean(scaled * normed, axis=-1, keepdims=True)
    )
    return (grad_in, jnp.sum(grad_out * normed, axis=0), jnp.sum(grad_out, axis=0))


def gelu_slope(u):
    return 0.5 * (1.0 + lax.erf(u / math.sqrt(2.0))) + u * jnp.exp(-0.5 * u * u) / math.sqrt(
        2.0 * math.pi
    )


def run_forward(layer_in, weights, keeps):
    (
        gain_one,
        shift_one,
        w_qkv,
        bias_qv,
        w_proj,
        b_proj,
        gain_two,
        shift_two,
        w_up,
        b_up,
        w_down,
        b_down,
    ) = weights
    images, length, width = layer_in.shape
    heads = width // HEAD_DIM
    rows = images * length
    scale = HEAD_DIM ** (-0.5)
    keep_attn = jnp.repeat(keeps[0], length)[:, None]
    keep_mlp = jnp.repeat(keeps[1], length)[:, None]
    h_rows = layer_in.astype(jnp.float32).reshape(rows, width)
    a_val, normed_one, factor_one = norm_parts(h_rows, gain_one, shift_one)
    a_low = a_val.astype(jnp.bfloat16)
    qkv = jnp.dot(a_low, w_qkv, preferred_element_type=jnp.float32)
    query = (
        (qkv[:, :width] + bias_qv[:width])
        .astype(jnp.bfloat16)
        .reshape(images, length, heads, HEAD_DIM)
    )
    keyed = qkv[:, width : 2 * width].astype(jnp.bfloat16).reshape(images, length, heads, HEAD_DIM)
    value = (
        (qkv[:, 2 * width :] + bias_qv[width:])
        .astype(jnp.bfloat16)
        .reshape(images, length, heads, HEAD_DIM)
    )
    scores = jnp.einsum("ishd,ithd->ihst", query, keyed, preferred_element_type=jnp.float32) * scale
    top = jnp.max(scores, axis=-1, keepdims=True)
    expd = jnp.exp(scores - top)
    probs = expd / jnp.sum(expd, axis=-1, keepdims=True)
    probs_low = probs.astype(jnp.bfloat16)
    attended = jnp.einsum("ihst,ithd->ishd", probs_low, value, preferred_element_type=jnp.float32)
    attended_low = attended.astype(jnp.bfloat16).reshape(rows, width)
    branch = jnp.dot(attended_low, w_proj, preferred_element_type=jnp.float32) + b_proj
    x_mid = h_rows + keep_attn * branch
    c_val, normed_two, factor_two = norm_parts(x_mid, gain_two, shift_two)
    c_low = c_val.astype(jnp.bfloat16)
    u_val = jnp.dot(c_low, w_up, preferred_element_type=jnp.float32) + b_up
    g_low = jax.nn.gelu(u_val, approximate=False).astype(jnp.bfloat16)
    mlp_out = jnp.dot(g_low, w_down, preferred_element_type=jnp.float32) + b_down
    x_end = x_mid + keep_mlp * mlp_out
    result = x_end.astype(jnp.bfloat16).reshape(images, length, width)
    saved = (
        normed_one,
        factor_one,
        a_low,
        query,
        keyed,
        value,
        probs,
        probs_low,
        attended_low,
        normed_two,
        factor_two,
        c_low,
        u_val,
        g_low,
        keep_attn,
        keep_mlp,
    )
    return (result, saved)


def run_backward(layer_in, weights, keeps, upstream):
    (
        gain_one,
        shift_one,
        w_qkv,
        bias_qv,
        w_proj,
        b_proj,
        gain_two,
        shift_two,
        w_up,
        b_up,
        w_down,
        b_down,
    ) = weights
    images, length, width = layer_in.shape
    heads = width // HEAD_DIM
    rows = images * length
    scale = HEAD_DIM ** (-0.5)
    (
        normed_one,
        factor_one,
        a_low,
        query,
        keyed,
        value,
        probs,
        probs_low,
        attended_low,
        normed_two,
        factor_two,
        c_low,
        u_val,
        g_low,
        keep_attn,
        keep_mlp,
    ) = run_forward(layer_in, weights, keeps)[1]
    d_end = upstream.astype(jnp.float32).reshape(rows, width)
    d_mlp = (d_end * keep_mlp).astype(jnp.bfloat16)
    grad_down = jnp.dot(g_low.T, d_mlp, preferred_element_type=jnp.float32)
    grad_down_bias = jnp.sum(d_mlp.astype(jnp.float32), axis=0)
    d_gel = jnp.dot(d_mlp, w_down.T, preferred_element_type=jnp.float32)
    d_up = (d_gel * gelu_slope(u_val)).astype(jnp.bfloat16)
    grad_up = jnp.dot(c_low.T, d_up, preferred_element_type=jnp.float32)
    grad_up_bias = jnp.sum(d_up.astype(jnp.float32), axis=0)
    d_c = jnp.dot(d_up, w_up.T, preferred_element_type=jnp.float32)
    d_mid_norm, grad_gain_two, grad_shift_two = norm_back(d_c, normed_two, factor_two, gain_two)
    d_mid = d_end + d_mid_norm
    d_branch = (d_mid * keep_attn).astype(jnp.bfloat16)
    grad_proj = jnp.dot(attended_low.T, d_branch, preferred_element_type=jnp.float32)
    grad_proj_bias = jnp.sum(d_branch.astype(jnp.float32), axis=0)
    d_att = jnp.dot(d_branch, w_proj.T, preferred_element_type=jnp.float32)
    d_att = d_att.astype(jnp.bfloat16).reshape(images, length, heads, HEAD_DIM)
    d_probs = jnp.einsum("ishd,ithd->ihst", d_att, value, preferred_element_type=jnp.float32)
    d_value = jnp.einsum("ihst,ishd->ithd", probs_low, d_att, preferred_element_type=jnp.float32)
    d_scores = probs * (d_probs - jnp.sum(d_probs * probs, axis=-1, keepdims=True))
    d_scores = d_scores.astype(jnp.bfloat16)
    d_query = (
        jnp.einsum("ihst,ithd->ishd", d_scores, keyed, preferred_element_type=jnp.float32) * scale
    )
    d_keyed = (
        jnp.einsum("ihst,ishd->ithd", d_scores, query, preferred_element_type=jnp.float32) * scale
    )
    d_qkv = jnp.concatenate(
        [d_query.reshape(rows, width), d_keyed.reshape(rows, width), d_value.reshape(rows, width)],
        axis=1,
    ).astype(jnp.bfloat16)
    grad_qkv = jnp.dot(a_low.T, d_qkv, preferred_element_type=jnp.float32)
    column_sums = jnp.sum(d_qkv.astype(jnp.float32), axis=0)
    grad_bias_qv = jnp.concatenate([column_sums[:width], column_sums[2 * width :]])
    d_a = jnp.dot(d_qkv, w_qkv.T, preferred_element_type=jnp.float32)
    d_in_norm, grad_gain_one, grad_shift_one = norm_back(d_a, normed_one, factor_one, gain_one)
    d_in = (d_mid + d_in_norm).astype(jnp.bfloat16).reshape(images, length, width)
    grads = (
        grad_gain_one,
        grad_shift_one,
        grad_qkv,
        grad_bias_qv,
        grad_proj,
        grad_proj_bias,
        grad_gain_two,
        grad_shift_two,
        grad_up,
        grad_up_bias,
        grad_down,
        grad_down_bias,
    )
    return (d_in, grads)


def per_device(
    inputs,
    ln1_gain,
    ln1_bias,
    qkv_weight,
    qv_bias,
    proj_weight,
    proj_bias,
    ln2_gain,
    ln2_bias,
    fc1_weight,
    fc1_bias,
    fc2_weight,
    fc2_bias,
    keep_masks,
    cotangent,
):
    weights = tuple(
        (
            w[0]
            for w in (
                ln1_gain,
                ln1_bias,
                qkv_weight,
                qv_bias,
                proj_weight,
                proj_bias,
                ln2_gain,
                ln2_bias,
                fc1_weight,
                fc1_bias,
                fc2_weight,
                fc2_bias,
            )
        )
    )
    section_index = lax.axis_index("section")
    first = section_index == 0
    micro = inputs.shape[0]
    keep_scaled = keep_masks[0].astype(jnp.float32) * survive

    def keeps_for(index):
        clipped = jnp.clip(index, 0, micro - 1)
        return lax.dynamic_index_in_dim(keep_scaled, clipped, 1, keepdims=False)

    received = jnp.zeros_like(inputs[0])
    kept_inputs = []
    results = []
    for tick in range(micro + 1):
        own = inputs[min(tick, micro - 1)]
        layer_in = jnp.where(first, own, received)
        kept_inputs.append(layer_in)
        result = run_forward(layer_in, weights, keeps_for(tick - section_index))[0]
        results.append(result)
        if tick < micro:
            received = from_behind(result, "section", 1)
    layer_outputs = jnp.where(first, jnp.stack(results[:micro]), jnp.stack(results[1:]))[None]
    returned = jnp.zeros_like(inputs[0])
    grads_in = []
    totals = None
    for tick in range(micro + 1):
        index = micro - tick - section_index
        valid = (index >= 0) & (index < micro)
        own = cotangent[max(micro - 1 - tick, 0)]
        upstream = jnp.where(first, returned, own)
        upstream = jnp.where(valid, upstream, jnp.zeros_like(upstream))
        d_in, grads = run_backward(kept_inputs[micro - tick], weights, keeps_for(index), upstream)
        grads_in.append(d_in)
        if tick < micro:
            returned = from_behind(d_in, "section", -1)
        totals = grads if totals is None else tuple((t + s for t, s in zip(totals, grads)))
    totals = lax.psum_scatter(totals, "dp", scatter_dimension=0, tiled=True)
    whole = jax.tree.map(
        lambda part, own: part.astype(own.dtype),
        lax.all_gather(as_sent(totals), "dp", axis=0, tiled=True),
        totals,
    )
    input_grads = jnp.where(
        first, jnp.stack(grads_in[1:][::-1]), jnp.stack(grads_in[:micro][::-1])
    )[None]
    return (
        layer_outputs,
        input_grads,
        whole[0][None],
        whole[1][None],
        whole[2][None],
        whole[3][None],
        whole[4][None],
        whole[5][None],
        whole[6][None],
        whole[7][None],
        whole[8][None],
        whole[9][None],
        whole[10][None],
        whole[11][None],
    )


def solution(mesh):
    in_specs = (
        P(None, "dp", None, None),
        P("section", None),
        P("section", None),
        P("section", None, None),
        P("section", None),
        P("section", None, None),
        P("section", None),
        P("section", None),
        P("section", None),
        P("section", None, None),
        P("section", None),
        P("section", None, None),
        P("section", None),
        P("section", None, None, "dp"),
        P(None, "dp", None, None),
    )
    out_specs = (
        P("section", None, "dp", None, None),
        P("section", None, "dp", None, None),
        P("section", None),
        P("section", None),
        P("section", None, None),
        P("section", None),
        P("section", None, None),
        P("section", None),
        P("section", None),
        P("section", None),
        P("section", None, None),
        P("section", None),
        P("section", None, None),
        P("section", None),
    )
    return jax.shard_map(
        per_device, mesh=mesh, in_specs=in_specs, out_specs=out_specs, check_vma=False
    )
```

profile of v0, /device:TPU:1, one launch (start us, length us, event | category | flops | bytes accessed | tf_op | source)
XLA Modules:
  0.0 938.3 jit_solution(14379263398732832753)
XLA Ops:
  7.3 5.8 fusion.559
  27.6 4.2 fusion.566
  36.6 3.6 fusion.60
  40.3 6.7 fusion.265
  47.0 4.2 collective-permute-start
  51.2 5.7 collective-permute-done
  65.8 4.2 fusion.568
  73.8 9.0 fusion.115
  84.9 4.4 collective-permute-start.1
  89.3 4.8 collective-permute-done.1
  103.0 4.2 fusion.570
  111.1 8.9 fusion.118
  122.0 4.6 collective-permute-start.2
  126.6 3.8 collective-permute-done.2
  139.2 4.1 fusion.572
  147.5 8.9 fusion.121
  156.5 2.6 fusion.274
  159.1 5.0 collective-permute-start.3
  164.1 2.9 fusion.558
  167.0 3.2 convert_reduce_fusion.19
  180.1 4.1 fusion.574
  188.4 9.0 fusion.124
  197.4 5.4 convert_reduce_fusion.4
  211.4 2.4 convolution_convert_fusion.4
  221.1 4.3 fusion.453
  228.8 3.7 convert_reduce_fusion.3
  232.6 2.4 multiply_reduce_fusion.13
  235.0 2.4 convert_reduce_fusion.23
  241.3 2.4 convolution_convert_fusion.3
  250.9 4.2 fusion.455
  258.6 3.9 convert_reduce_fusion.2
  264.9 2.4 convert_reduce_fusion.22
  271.3 2.4 convolution_convert_fusion.2
  280.5 4.4 fusion.457
  288.4 3.7 convert_reduce_fusion.1
  294.5 2.4 convert_reduce_fusion.21
  300.8 2.4 convolution_convert_fusion.1
  311.5 5.3 collective-permute-done.7
  318.2 3.4 convert_reduce_fusion
  324.0 2.5 convert_reduce_fusion.20
  329.9 5.7 fusion.459
  338.8 2.6 multiply_reduce_fusion
  346.4 11.7 %add_add_fusion.2 = f32[768,2304]{1,0:T(8,128)} fusion(f32[768,2304]{1,0:T(8,128)} %fusion.459, f32[768,2304]{1,0:T(8,128)} %fusion.457, f32[768,2304]{1,0:T(8,128)S(1)} %bitcast.798, f32[768,2304]{1,0:T(8,128)} %fusion.455, bf16[1,1,198,768]{3,2,1,0:T(8,128)(2,1)S(1)} %copy-done.27, f32[768]{0:T(1024)S(1)} %reduce.36, f32[198]{0:T(256)S(1)} %copy-done.215, ...), kind=kOutput, calls=%fused_computation.7 | convolution fusion | flops 711438336 | bytes 36613680 | tf_op jit(solution)/shard_map/dot_general | solution.py:194
  358.8 6.9 fusion.545
  365.7 5.1 fusion.544
  370.9 5.3 fusion.543
  376.3 5.3 fusion.542
  381.6 17.4 %add_add_fusion.1 = f32[768,3072]{1,0:T(8,128)} fusion(f32[768,3072]{1,0:T(8,128)} %fusion.542, f32[768,3072]{1,0:T(8,128)} %fusion.543, f32[768,3072]{1,0:T(8,128)} %fusion.545, f32[768,3072]{1,0:T(8,128)} %fusion.544, bf16[198,3072]{1,0:T(8,128)(2,1)S(1)} %copy-done.132, f32[198,768]{1,0:T(8,128)S(1)} %copy-done.12, f32[768]{0:T(1024)S(1)} %reduce.41, ...), kind=kOutput, calls=%fused_computation.6 | convolution fusion | flops 944478720 | bytes 49018416 | tf_op jit(solution)/shard_map/dot_general | solution.py:170
  399.5 7.3 fusion.515
  406.9 6.2 fusion.522
  413.1 6.2 fusion.520
  419.3 6.2 fusion.518
  425.5 21.8 %add_add_fusion = f32[3072,768]{1,0:T(8,128)} fusion(f32[3072,768]{1,0:T(8,128)} %fusion.518, f32[3072,768]{1,0:T(8,128)} %fusion.520, f32[3072,768]{1,0:T(8,128)} %fusion.515, f32[3072,768]{1,0:T(8,128)} %fusion.522, bf16[1,198,768]{2,1,0:T(8,128)(2,1)S(1)} %copy-done.149, f32[]{:T(128)} %bitcast.11, f32[198,3072]{1,0:T(8,128)} %copy-done.80), kind=kOutput, calls=%fused_computation.5 | convolution fusion | flops 983711232 | bytes 49923076 | tf_op jit(solution)/shard_map/dot_general | solution.py:166
  449.0 44.6 %reduce-scatter.5.cloned.1.call-done = f32[48,2304]{1,0:T(8,128)} async-done(((f32[768,2304]{1,0:T(8,128)}), f32[48,2304]{1,0:T(8,128)}) %reduce-scatter.5.cloned.1.call-update) | async-done | bytes 442384 | tf_op jit(solution)/shard_map/reduce_scatter | solution.py:288
  495.4 114.0 %reduce-scatter.9.cloned.1.call-done = f32[48,3072]{1,0:T(8,128)} async-done(((f32[768,3072]{1,0:T(8,128)}), f32[48,3072]{1,0:T(8,128)}) %reduce-scatter.9.cloned.1.call-update) | async-done | bytes 589840 | tf_op jit(solution)/shard_map/reduce_scatter | solution.py:288
  611.5 113.4 %reduce-scatter.11.cloned.1.call-done = f32[192,768]{1,0:T(8,128)} async-done(((f32[3072,768]{1,0:T(8,128)}), f32[192,768]{1,0:T(8,128)}) %reduce-scatter.11.cloned.1.call-update) | async-done | bytes 589840 | tf_op jit(solution)/shard_map/reduce_scatter | solution.py:288
  732.9 4.9 fusion.280
  750.4 58.2 %all-reduce.16 = (bf16[768]{0:T(1024)(128)(2,1)}, bf16[768]{0:T(1024)(128)(2,1)}, bf16[1536]{0:T(1024)(128)(2,1)}, bf16[768]{0:T(1024)(128)(2,1)}, bf16[768]{0:T...) all-reduce(f32[768]{0:T(1024)} %get-tuple-element.252, ...), channel_id=2, replica_groups=mesh['section'=2,'dp'=16] {'dp'}, use_global_device_ids=true, to_apply=%region_60.61.clone | all-reduce | flops 9216 | bytes 55296
  823.1 59.5 %all-reduce.17 = (bf16[768]{0:T(1024)(128)(2,1)}, bf16[768]{0:T(1024)(128)(2,1)}, bf16[1536]{0:T(1024)(128)(2,1)}, bf16[768]{0:T(1024)(128)(2,1)}, bf16[768]{0:T...) all-reduce(bf16[768]{0:T(1024)(128)(2,1)} %copy-done.255, ...), channel_id=1, replica_groups=mesh['section'=2,'dp'=16] {'dp'}, use_global_device_ids=true, to_apply=%add | all-reduce | flops 9216 | bytes 36864
  892.6 2.8 bitcast_convert_fusion.3
  895.5 5.5 bitcast_convert_fusion.2
  901.0 7.4 bitcast_convert_fusion.1
  908.4 16.1 %all-gather.11.cloned.1.call-done = bf16[3072,768]{1,0:T(8,128)(2,1)} async-done(((bf16[192,768]{1,0:T(8,128)(2,1)}), bf16[3072,768]{1,0:T(8,128)(2,1)}) %all-gather.11.cloned.1.call-update) | async-done | bytes 4718608 | tf_op jit(solution)/shard_map/all_gather | solution.py:291
  924.4 6.8 bitcast_convert_fusion
  (892 shorter events, 201.3 us)
Async XLA Ops:
  7.2 8.8 copy-start
  7.2 440.1 %reduce-scatter.7.cloned.1.call-start = ((), (), s32[]{:S(2)}) async-start(), calls=%async_computation.6 | async-start | bytes 2506752 | tf_op jit(solution)/shard_map/reduce_scatter | solution.py:288
  17.0 8.6 copy-start.285
  40.3 16.7 %copy-start.95 = (bf16[1,1,198,768]{3,0,2,1:T(2,128)(2,1)S(1)}, bf16[1,1,198,768]{3,0,2,1:T(2,128)(2,1)}, u32[]{:S(2)}) copy-start(bf16[1,1,198,768]{3,0,2,1:T(2,128)(2,1)} %get-tuple-element.165) | copy-start | bytes 912388
  47.0 11.4 %copy-start.159 = (bf16[198,768]{1,0:T(8,128)(2,1)}, bf16[198,768]{1,0:T(8,128)(2,1)S(1)}, u32[]{:S(2)}) copy-start(bf16[198,768]{1,0:T(8,128)(2,1)S(1)} %fusion.265) | copy-start | bytes 912388
  47.0 9.9 %collective-permute-start = (bf16[1,198,768]{2,1,0:T(8,128)(2,1)S(1)}, bf16[1,198,768]{2,1,0:T(8,128)(2,1)S(1)}, u32[]{:S(2)}, u32[]{:S(2)}) collective-permute-start(bf16[1,198,768]{2,1,0:T(8,128)(2,1)S(1)} %bitcast.912), channel_id=1, source_target_pairs={{0,16},{1,17},{2,18},{3,19},{4,20},{5,21},{6,22},{7,23},{8,24},{9,... | collective-permute-start | bytes 912392 | tf_op jit(solution)/shard_map/ppermute | solution.py:18
  72.2 10.6 %slice-start.14 = ((s8[4718592]{0:T(1024)(128)(4,1)}), s8[4194304]{0:T(1024)(128)(4,1)S(1)}, s32[]{:S(2)}) async-start(s8[4718592]{0:T(1024)(128)(4,1)} %bitcast.926), calls=%async_computation.26 | async-start | bytes 8388608
  73.5 9.3 copy-start.29
  73.5 9.3 copy-start.195
  73.8 9.0 copy-start.225
  73.8 9.0 copy-start.278
  73.8 9.0 slice-start.15
  82.9 11.2 %copy-start.94 = (bf16[1,1,198,768]{3,0,2,1:T(2,128)(2,1)S(1)}, bf16[1,1,198,768]{3,0,2,1:T(2,128)(2,1)}, u32[]{:S(2)}) copy-start(bf16[1,1,198,768]{3,0,2,1:T(2,128)(2,1)} %get-tuple-element.164) | copy-start | bytes 912388
  84.9 10.7 %copy-start.161 = (bf16[198,768]{1,0:T(8,128)(2,1)}, bf16[198,768]{1,0:T(8,128)(2,1)S(1)}, u32[]{:S(2)}) copy-start(bf16[198,768]{1,0:T(8,128)(2,1)S(1)} %fusion.268) | copy-start | bytes 912388
  84.9 9.2 collective-permute-start.1
  109.5 10.6 %slice-start.16 = ((s8[4718592]{0:T(1024)(128)(4,1)}), s8[4194304]{0:T(1024)(128)(4,1)S(1)}, s32[]{:S(2)}) async-start(s8[4718592]{0:T(1024)(128)(4,1)} %bitcast.928), calls=%async_computation.28 | async-start | bytes 8388608
  110.8 9.2 copy-start.33
  110.8 9.2 copy-start.198
  111.1 9.0 copy-start.228
  111.1 9.0 copy-start.279
  111.1 9.0 slice-start.17
  120.1 10.2 %copy-start.43 = (bf16[1,1,198,768]{3,0,2,1:T(2,128)(2,1)S(1)}, bf16[1,1,198,768]{3,0,2,1:T(2,128)(2,1)}, u32[]{:S(2)}) copy-start(bf16[1,1,198,768]{3,0,2,1:T(2,128)(2,1)} %get-tuple-element.163) | copy-start | bytes 912388
  122.0 9.8 %copy-start.163 = (bf16[198,768]{1,0:T(8,128)(2,1)}, bf16[198,768]{1,0:T(8,128)(2,1)S(1)}, u32[]{:S(2)}) copy-start(bf16[198,768]{1,0:T(8,128)(2,1)S(1)} %fusion.271) | copy-start | bytes 912388
  122.0 8.4 collective-permute-start.2
  143.3 13.1 %slice-start.18 = ((s8[4718592]{0:T(1024)(128)(4,1)}), s8[4194304]{0:T(1024)(128)(4,1)S(1)}, s32[]{:S(2)}) async-start(s8[4718592]{0:T(1024)(128)(4,1)} %bitcast.930), calls=%async_computation.30 | async-start | bytes 8388608
  147.2 9.3 copy-start.36
  147.2 9.2 copy-start.201
  147.4 9.0 copy-start.231
  147.5 9.0 copy-start.280
  147.5 9.0 slice-start.19
  159.1 11.0 %collective-permute-start.3 = (bf16[1,198,768]{2,1,0:T(8,128)(2,1)}, bf16[1,198,768]{2,1,0:T(8,128)(2,1)}, u32[]{:S(2)}, u32[]{:S(2)}) collective-permute-start(bf16[1,198,768]{2,1,0:T(8,128)(2,1)} %bitcast.55), channel_id=1, source_target_pairs={{0,16},{1,17},{2,18},{3,19},{4,20},{5,21},{6,22},{7,23},{8,24},{9,... | collective-permute-start | bytes 912392 | tf_op jit(solution)/shard_map/ppermute | solution.py:18
  184.2 18.6 %slice-start.2 = ((s8[4718592]{0:T(1024)(128)(4,1)}), s8[4194304]{0:T(1024)(128)(4,1)S(1)}, s32[]{:S(2)}) async-start(s8[4718592]{0:T(1024)(128)(4,1)} %bitcast.799), calls=%async_computation.14 | async-start | bytes 8388608
  188.1 17.1 %copy-start.32 = (f32[198,768]{1,0:T(8,128)}, f32[198,768]{1,0:T(8,128)S(1)}, u32[]{:S(2)}) copy-start(f32[198,768]{1,0:T(8,128)S(1)} %get-tuple-element.214) | copy-start | bytes 1824772
  188.1 17.1 %copy-start.204 = (f32[198]{0:T(256)}, f32[198]{0:T(256)S(1)}, u32[]{:S(2)}) copy-start(f32[198]{0:T(256)S(1)} %broadcast_multiply_fusion.20) | copy-start | bytes 2380
  188.3 16.9 %copy-start.234 = (f32[198]{0:T(256)}, f32[198]{0:T(256)S(1)}, u32[]{:S(2)}) copy-start(f32[198]{0:T(256)S(1)} %add_rsqrt_fusion) | copy-start | bytes 2380
  188.4 9.0 copy-start.69
  188.4 14.5 %slice-start.3 = ((s8[4718592]{0:T(1024)(128)(4,1)}), s8[524288]{0:T(1024)(128)(4,1)S(1)}, s32[]{:S(2)}) async-start(s8[4718592]{0:T(1024)(128)(4,1)} %bitcast.799), calls=%async_computation.15 | async-start | bytes 1048576
  214.8 14.0 %slice-start.20 = ((s8[4718592]{0:T(1024)(128)(4,1)}), s8[4194304]{0:T(1024)(128)(4,1)S(1)}, s32[]{:S(2)}) async-start(s8[4718592]{0:T(1024)(128)(4,1)} %bitcast.932), calls=%async_computation.32 | async-start | bytes 8388608
  217.3 11.5 %slice-start.21 = ((s8[4718592]{0:T(1024)(128)(4,1)}), s8[524288]{0:T(1024)(128)(4,1)S(1)}, s32[]{:S(2)}) async-start(s8[4718592]{0:T(1024)(128)(4,1)} %bitcast.932), calls=%async_computation.33 | async-start | bytes 1048576
  219.6 7.7 collective-permute-start.4
  221.1 11.5 %slice-start.4 = ((s8[4718592]{0:T(1024)(128)(4,1)}), s8[4194304]{0:T(1024)(128)(4,1)S(1)}, s32[]{:S(2)}) async-start(s8[4718592]{0:T(1024)(128)(4,1)} %bitcast.801), calls=%async_computation.16 | async-start | bytes 8388608
  244.6 13.9 %slice-start.22 = ((s8[4718592]{0:T(1024)(128)(4,1)}), s8[4194304]{0:T(1024)(128)(4,1)S(1)}, s32[]{:S(2)}) async-start(s8[4718592]{0:T(1024)(128)(4,1)} %bitcast.934), calls=%async_computation.34 | async-start | bytes 8388608
  247.1 11.4 %slice-start.23 = ((s8[4718592]{0:T(1024)(128)(4,1)}), s8[524288]{0:T(1024)(128)(4,1)S(1)}, s32[]{:S(2)}) async-start(s8[4718592]{0:T(1024)(128)(4,1)} %bitcast.934), calls=%async_computation.35 | async-start | bytes 1048576
  249.5 7.7 collective-permute-start.5
  250.9 11.5 %slice-start.6 = ((s8[4718592]{0:T(1024)(128)(4,1)}), s8[4194304]{0:T(1024)(128)(4,1)S(1)}, s32[]{:S(2)}) async-start(s8[4718592]{0:T(1024)(128)(4,1)} %bitcast.803), calls=%async_computation.18 | async-start | bytes 8388608
  278.9 9.5 %slice-start.24 = ((s8[4718592]{0:T(1024)(128)(4,1)}), s8[4194304]{0:T(1024)(128)(4,1)S(1)}, s32[]{:S(2)}) async-start(s8[4718592]{0:T(1024)(128)(4,1)} %bitcast.936), calls=%async_computation.36 | async-start | bytes 8388608
  278.9 8.0 copy-start.41
  278.9 9.4 %slice-start.25 = ((s8[4718592]{0:T(1024)(128)(4,1)}), s8[524288]{0:T(1024)(128)(4,1)S(1)}, s32[]{:S(2)}) async-start(s8[4718592]{0:T(1024)(128)(4,1)} %bitcast.936), calls=%async_computation.37 | async-start | bytes 1048576
  278.9 9.4 %copy-start.287 = (f32[198,3072]{1,0:T(8,128)S(1)}, f32[198,3072]{1,0:T(8,128)}, u32[]{:S(2)}) copy-start(f32[198,3072]{1,0:T(8,128)} %get-tuple-element.198) | copy-start | bytes 7299076
  278.9 8.0 collective-permute-start.6
  280.5 11.6 %slice-start.8 = ((s8[4718592]{0:T(1024)(128)(4,1)}), s8[4194304]{0:T(1024)(128)(4,1)S(1)}, s32[]{:S(2)}) async-start(s8[4718592]{0:T(1024)(128)(4,1)} %bitcast.805), calls=%async_computation.20 | async-start | bytes 8388608
  304.2 13.9 %slice-start.26 = ((s8[4718592]{0:T(1024)(128)(4,1)}), s8[4194304]{0:T(1024)(128)(4,1)S(1)}, s32[]{:S(2)}) async-start(s8[4718592]{0:T(1024)(128)(4,1)} %bitcast.938), calls=%async_computation.38 | async-start | bytes 8388608
  306.7 11.4 %slice-start.27 = ((s8[4718592]{0:T(1024)(128)(4,1)}), s8[524288]{0:T(1024)(128)(4,1)S(1)}, s32[]{:S(2)}) async-start(s8[4718592]{0:T(1024)(128)(4,1)} %bitcast.938), calls=%async_computation.39 | async-start | bytes 1048576
  309.1 7.7 collective-permute-start.7
  310.5 11.1 %slice-start.10 = ((s8[4718592]{0:T(1024)(128)(4,1)}), s8[4194304]{0:T(1024)(128)(4,1)S(1)}, s32[]{:S(2)}) async-start(s8[4718592]{0:T(1024)(128)(4,1)} %bitcast.807), calls=%async_computation.22 | async-start | bytes 8388608
  329.6 164.0 %reduce-scatter.5.cloned.1.call-start = ((), (), s32[]{:S(2)}) async-start(), calls=%async_computation.4 | async-start | bytes 7520256 | tf_op jit(solution)/shard_map/reduce_scatter | solution.py:288
  358.1 251.3 %reduce-scatter.9.cloned.1.call-start = ((), (), s32[]{:S(2)}) async-start(), calls=%async_computation.8 | async-start | bytes 10027008 | tf_op jit(solution)/shard_map/reduce_scatter | solution.py:288
  399.0 325.8 %reduce-scatter.11.cloned.1.call-start = ((), (), s32[]{:S(2)}) async-start(), calls=%async_computation.10 | async-start | bytes 10027008 | tf_op jit(solution)/shard_map/reduce_scatter | solution.py:288
  447.3 279.4 %copy-start.286 = (u32[32]{0:T(128)S(1)}, u32[32]{0:T(128)}, u32[]{:S(2)}) copy-start(u32[32]{0:T(128)} %constant.194) | copy-start | bytes 388
  447.3 285.5 %copy-start.281 = (f32[768]{0:T(1024)S(1)}, f32[768]{0:T(1024)}, u32[]{:S(2)}) copy-start(f32[768]{0:T(1024)} %reduce.42) | copy-start | bytes 9220
  447.3 445.3 %all-gather.7.cloned.1.call-start = ((), (), s32[]{:S(2)}) async-start(), calls=%async_computation.7 | async-start | bytes 1253376 | tf_op jit(solution)/shard_map/all_gather | solution.py:291
  448.9 446.5 %all-gather.5.cloned.1.call-start = ((), (), s32[]{:S(2)}) async-start(), calls=%async_computation.5 | async-start | bytes 3760128 | tf_op jit(solution)/shard_map/all_gather | solution.py:291
  495.4 405.6 %all-gather.9.cloned.1.call-start = ((), (), s32[]{:S(2)}) async-start(), calls=%async_computation.9 | async-start | bytes 5013504 | tf_op jit(solution)/shard_map/all_gather | solution.py:291
  611.3 313.2 %all-gather.11.cloned.1.call-start = ((), (), s32[]{:S(2)}) async-start(), calls=%async_computation.11 | async-start | bytes 5013504 | tf_op jit(solution)/shard_map/all_gather | solution.py:291
  (270 other events, 886.9 us)
Sparse Core Ops, SparseCore 0:
  329.7 69.0 reduce-scatter.6
  403.4 90.1 reduce-scatter.4
  498.3 111.1 reduce-scatter.8
  614.0 110.8 reduce-scatter.10
  727.6 38.6 all-gather.6
  769.0 46.0 all-gather.4
  817.9 52.3 all-gather.8
  872.6 51.7 all-gather.10
where the time goes:
time: 951 us; the launch traced here: 938 us
  waiting for transfers between devices  310 us (33%)
  matrix products  294 us (31%)
  blocking collectives  118 us (12%)
  local copies, waits for them, and re-layouts  92.6 us (10%)
  other arithmetic  76.9 us (8%)
  starting transfers between devices  25.1 us (3%)
  between operations  22 us (2%)
    reduce_scatter x4, waiting for transfers between devices, per_device(): totals = lax.psum_scatter(totals, 'dp', scatter_dimension=0, tiled=True)  272 us
    unnamed x2, blocking collectives  118 us
    dot_general x5, matrix products, run_backward(): grad_down = jnp.dot(g_low.T, d_mlp, preferred_element_type=jnp.float32)  47.7 us
    dot_general x5, matrix products, run_backward(): grad_up = jnp.dot(c_low.T, d_up, preferred_element_type=jnp.float32)  40.1 us
    dot_general x5, matrix products, run_forward(): u_val = jnp.dot(c_low, w_up, preferred_element_type=jnp.float32) + b_up  39.4 us
    unnamed x663, local copies, waits for them, and re-layouts  32.1 us
    dot_general x5, matrix products, run_backward(): grad_qkv = jnp.dot(a_low.T, d_qkv, preferred_element_type=jnp.float32)  30.4 us
    ppermute x8, starting transfers between devices, from_behind(): lax.ppermute(value, axis, [(source, source + steps) for source in range(i...  24 us
  transfers between devices with their start and end apart: 16, of which 11 were waited for; matrix products, arithmetic and copies ran while one was open for 22% of the time, Pallas kernels for 0%

commit v1 on v0

--- a/solution.py
+++ b/solution.py
@@ -1,8 +1,11 @@
+import functools
 import math
 
 import jax
 import jax.numpy as jnp
 from jax import lax
+from jax.experimental import pallas as pl
+from jax.experimental.pallas import tpu as pltpu
 from jax.sharding import PartitionSpec as P
 
 HEAD_DIM = 64
@@ -163,17 +166,14 @@
     ) = run_forward(layer_in, weights, keeps)[1]
     d_end = upstream.astype(jnp.float32).reshape(rows, width)
     d_mlp = (d_end * keep_mlp).astype(jnp.bfloat16)
-    grad_down = jnp.dot(g_low.T, d_mlp, preferred_element_type=jnp.float32)
     grad_down_bias = jnp.sum(d_mlp.astype(jnp.float32), axis=0)
     d_gel = jnp.dot(d_mlp, w_down.T, preferred_element_type=jnp.float32)
     d_up = (d_gel * gelu_slope(u_val)).astype(jnp.bfloat16)
-    grad_up = jnp.dot(c_low.T, d_up, preferred_element_type=jnp.float32)
     grad_up_bias = jnp.sum(d_up.astype(jnp.float32), axis=0)
     d_c = jnp.dot(d_up, w_up.T, preferred_element_type=jnp.float32)
     d_mid_norm, grad_gain_two, grad_shift_two = norm_back(d_c, normed_two, factor_two, gain_two)
     d_mid = d_end + d_mid_norm
     d_branch = (d_mid * keep_attn).astype(jnp.bfloat16)
-    grad_proj = jnp.dot(attended_low.T, d_branch, preferred_element_type=jnp.float32)
     grad_proj_bias = jnp.sum(d_branch.astype(jnp.float32), axis=0)
     d_att = jnp.dot(d_branch, w_proj.T, preferred_element_type=jnp.float32)
     d_att = d_att.astype(jnp.bfloat16).reshape(images, length, heads, HEAD_DIM)
@@ -191,27 +191,360 @@
         [d_query.reshape(rows, width), d_keyed.reshape(rows, width), d_value.reshape(rows, width)],
         axis=1,
     ).astype(jnp.bfloat16)
-    grad_qkv = jnp.dot(a_low.T, d_qkv, preferred_element_type=jnp.float32)
     column_sums = jnp.sum(d_qkv.astype(jnp.float32), axis=0)
     grad_bias_qv = jnp.concatenate([column_sums[:width], column_sums[2 * width :]])
     d_a = jnp.dot(d_qkv, w_qkv.T, preferred_element_type=jnp.float32)
     d_in_norm, grad_gain_one, grad_shift_one = norm_back(d_a, normed_one, factor_one, gain_one)
     d_in = (d_mid + d_in_norm).astype(jnp.bfloat16).reshape(images, length, width)
-    grads = (
+    small = (
         grad_gain_one,
         grad_shift_one,
-        grad_qkv,
         grad_bias_qv,
-        grad_proj,
         grad_proj_bias,
         grad_gain_two,
         grad_shift_two,
-        grad_up,
         grad_up_bias,
-        grad_down,
         grad_down_bias,
     )
-    return (d_in, grads)
+    left = jnp.concatenate([a_low, attended_low, c_low, g_low], axis=1)
+    right = jnp.concatenate([d_qkv, d_branch, d_up, d_mlp], axis=1)
+    return (d_in, left, right, jnp.concatenate(small))
+
+
+COLS = 256
+SLOTS = 8
+LAST = 7
+
+
+def reduce_kernel(
+    count,
+    width,
+    hidden,
+    left_ref,
+    right_ref,
+    small_ref,
+    qkv_ref,
+    proj_ref,
+    up_ref,
+    down_ref,
+    small_out,
+    partial,
+    give,
+    give_x,
+    give_z,
+    take,
+    take_x,
+    take_z,
+    whole,
+    sent_core,
+    sent_x,
+    sent_z,
+    spread_z,
+    spread_x,
+    spread_core,
+    got_core,
+    got_x,
+    got_z,
+    held_z,
+    held_x,
+    held_core,
+    out_sem,
+):
+    line = count // 4
+    per = width // COLS
+    up_chunks = hidden // COLS
+    first_proj, first_up = (3 * per, 4 * per)
+    first_down = first_up + up_chunks
+    chunks = first_down + per * (hidden // width)
+    me = lax.axis_index("dp")
+    core = lax.rem(me, 2)
+    chip = me // 2
+    across = lax.rem(chip, 2)
+    along = chip // 2
+    half = 2 * line
+
+    def device(z, x, k):
+        return {"dp": (z * 2 + x) * 2 + k}
+
+    other_core = device(along, across, 1 - core)
+    other_x = device(along, 1 - across, core)
+    others_z = [device(lax.rem(along + i, line), across, core) for i in range(1, line)]
+
+    barrier = pltpu.get_barrier_semaphore()
+    for peer in [other_core, other_x] + others_z:
+        pl.semaphore_signal(barrier, inc=1, device_id=peer, device_id_type=pl.DeviceIdType.MESH)
+    pl.semaphore_wait(barrier, 1 + line)
+
+    own_half = core * half
+    own_quarter = own_half + across * line
+    own_piece = own_quarter + along
+
+    def remote(src, dst, send, recv, peer):
+        return pltpu.make_async_remote_copy(
+            src_ref=src,
+            dst_ref=dst,
+            send_sem=send,
+            recv_sem=recv,
+            device_id=peer,
+            device_id_type=pl.DeviceIdType.MESH,
+        )
+
+    def to_core(s):
+        return remote(give.at[s], take.at[s], sent_core.at[s], got_core.at[s], other_core)
+
+    def to_x(s):
+        return remote(give_x.at[s], take_x.at[s], sent_x.at[s], got_x.at[s], other_x)
+
+    def to_z(s):
+        return [
+            remote(
+                give_z.at[s, lax.rem(along + i, line)],
+                take_z.at[s, i - 1],
+                sent_z.at[s, i - 1],
+                got_z.at[s, i - 1],
+                others_z[i - 1],
+            )
+            for i in range(1, line)
+        ]
+
+    def back_z(s):
+        piece = whole.at[s, own_piece]
+        return [
+            remote(
+                piece, piece, spread_z.at[s, i - 1], held_z.at[s, i - 1], others_z[i - 1]
+            )
+            for i in range(1, line)
+        ]
+
+    def back_x(s):
+        part = whole.at[s, pl.ds(own_quarter, line)]
+        return remote(part, part, spread_x.at[s], held_x.at[s], other_x)
+
+    def back_core(s):
+        part = whole.at[s, pl.ds(own_half, half)]
+        return remote(part, part, spread_core.at[s], held_core.at[s], other_core)
+
+    def for_output(u, s, act):
+        def go(ref, row, column):
+            columns = pl.ds(pl.multiple_of(column * COLS, COLS), COLS)
+            dst = ref.at[:, :, columns] if row is None else ref.at[row, :, :, columns]
+            act(pltpu.make_async_copy(whole.at[s], dst, out_sem.at[s]))
+
+        @pl.when(u < first_proj)
+        def _():
+            go(qkv_ref, None, u)
+
+        @pl.when((u >= first_proj) & (u < first_up))
+        def _():
+            go(proj_ref, None, u - first_proj)
+
+        @pl.when((u >= first_up) & (u < first_down))
+        def _():
+            go(up_ref, None, u - first_up)
+
+        @pl.when((u >= first_down) & (u < chunks))
+        def _():
+            go(down_ref, (u - first_down) // per, lax.rem(u - first_down, per))
+
+        @pl.when(u == chunks)
+        def _():
+            go(small_out, None, 0)
+
+    def step(t, carry):
+        def stage(delay):
+            u = t - delay
+            return u, lax.rem(u + SLOTS, SLOTS), (u >= 0) & (u <= chunks)
+
+        u7, s7, on7 = stage(7)
+
+        @pl.when(on7)
+        def _():
+            for_output(u7, s7, lambda copy: copy.wait())
+            to_core(s7).wait_send()
+            to_x(s7).wait_send()
+            for copy in to_z(s7) + back_z(s7):
+                copy.wait_send()
+            back_x(s7).wait_send()
+            back_core(s7).wait_send()
+
+        u6, s6, on6 = stage(6)
+
+        @pl.when(on6)
+        def _():
+            back_core(s6).wait_recv()
+            for_output(u6, s6, lambda copy: copy.start())
+
+        u5, s5, on5 = stage(5)
+
+        @pl.when(on5)
+        def _():
+            back_x(s5).wait_recv()
+            back_core(s5).start()
+
+        u4, s4, on4 = stage(4)
+
+        @pl.when(on4)
+        def _():
+            for copy in back_z(s4):
+                copy.wait_recv()
+            back_x(s4).start()
+
+        u3, s3, on3 = stage(3)
+
+        @pl.when(on3)
+        def _():
+            for copy in to_z(s3):
+                copy.wait_recv()
+            total = partial[s3, own_piece]
+            for i in range(line - 1):
+                total = total + take_z[s3, i].astype(jnp.float32)
+            whole[s3, own_piece] = total.astype(jnp.bfloat16)
+            for copy in back_z(s3):
+                copy.start()
+
+        u2, s2, on2 = stage(2)
+
+        @pl.when(on2)
+        def _():
+            to_x(s2).wait_recv()
+            quarter = pl.ds(own_quarter, line)
+            total = partial[s2, quarter] + take_x[s2].astype(jnp.float32)
+            partial[s2, quarter] = total
+            give_z[s2] = total.astype(jnp.bfloat16)
+            for copy in to_z(s2):
+                copy.start()
+
+        u1, s1, on1 = stage(1)
+
+        @pl.when(on1)
+        def _():
+            to_core(s1).wait_recv()
+            mine = pl.ds(own_half, half)
+            partial[s1, mine] = partial[s1, mine] + take[s1].astype(jnp.float32)
+            give_x[s1] = partial[s1, pl.ds(own_half + (1 - across) * line, line)].astype(
+                jnp.bfloat16
+            )
+            to_x(s1).start()
+
+        u0, s0, on0 = stage(0)
+
+        @pl.when(on0)
+        def _():
+            @pl.when(u0 < chunks)
+            def _():
+                def reached(k):
+                    return (u0 + chunks - k) // chunks
+
+                block = reached(first_proj) + reached(first_up)
+                for row in range(hidden // width):
+                    block = block + reached(first_down + per * row)
+                column = u0
+                for row in range(1, hidden // width):
+                    column = column - per * reached(first_down + per * row)
+                rows = pl.ds(pl.multiple_of(block * width, width), width)
+                columns = pl.ds(pl.multiple_of(column * COLS, COLS), COLS)
+                product = lax.dot_general(
+                    left_ref[:, rows],
+                    right_ref[:, columns],
+                    (((0,), (0,)), ((), ())),
+                    preferred_element_type=jnp.float32,
+                )
+                partial[s0] = product.reshape(partial.shape[1:])
+
+            @pl.when(u0 == chunks)
+            def _():
+                partial[s0] = small_ref[...]
+
+            give[s0] = partial[s0, pl.ds((1 - core) * half, half)].astype(jnp.bfloat16)
+            to_core(s0).start()
+
+        return carry
+
+    lax.fori_loop(0, chunks + 1 + LAST, step, 0)
+
+
+def sum_weight_grads(lefts, rights, small, width):
+    count = lax.axis_size("dp")
+    hidden = rights.shape[1] - 5 * width
+    piece = width // count
+    if width % COLS or count % 4 or width % (16 * count) or small.size > width * COLS:
+        return sum_weight_grads_plain(lefts, rights, small, width)
+    line = count // 4
+    tile = (count, piece, COLS)
+    small_in = jnp.pad(small, (0, width * COLS - small.size)).reshape(tile)
+    low, dma = (jnp.bfloat16, pltpu.SemaphoreType.DMA)
+    anywhere = pl.BlockSpec(memory_space=pl.ANY)
+    vmem = pl.BlockSpec(memory_space=pltpu.VMEM)
+    outs = pl.pallas_call(
+        functools.partial(reduce_kernel, count, width, hidden),
+        out_shape=(
+            jax.ShapeDtypeStruct((count, piece, 3 * width), low),
+            jax.ShapeDtypeStruct((count, piece, width), low),
+            jax.ShapeDtypeStruct((count, piece, hidden), low),
+            jax.ShapeDtypeStruct((hidden // width, count, piece, width), low),
+            jax.ShapeDtypeStruct(tile, low),
+        ),
+        in_specs=[vmem, vmem, vmem],
+        out_specs=(anywhere,) * 5,
+        scratch_shapes=[
+            pltpu.VMEM((SLOTS, count, piece, COLS), jnp.float32),
+            pltpu.VMEM((SLOTS, 2 * line, piece, COLS), low),
+            pltpu.VMEM((SLOTS, line, piece, COLS), low),
+            pltpu.VMEM((SLOTS, line, piece, COLS), low),
+            pltpu.VMEM((SLOTS, 2 * line, piece, COLS), low),
+            pltpu.VMEM((SLOTS, line, piece, COLS), low),
+            pltpu.VMEM((SLOTS, line - 1, piece, COLS), low),
+            pltpu.VMEM((SLOTS, count, piece, COLS), low),
+            dma((SLOTS,)),
+            dma((SLOTS,)),
+            dma((SLOTS, line - 1)),
+            dma((SLOTS, line - 1)),
+            dma((SLOTS,)),
+            dma((SLOTS,)),
+            dma((SLOTS,)),
+            dma((SLOTS,)),
+            dma((SLOTS, line - 1)),
+            dma((SLOTS, line - 1)),
+            dma((SLOTS,)),
+            dma((SLOTS,)),
+            dma((SLOTS,)),
+        ],
+        compiler_params=pltpu.CompilerParams(
+            collective_id=0, has_side_effects=True, vmem_limit_bytes=60 * 1024 * 1024
+        ),
+    )(lefts, rights, small_in)
+    qkv, proj, up, down, small_sum = (out.astype(jnp.float32) for out in outs)
+    return (
+        qkv.reshape(width, 3 * width),
+        proj.reshape(width, width),
+        up.reshape(width, hidden),
+        down.reshape(hidden, width),
+        small_sum.reshape(-1)[: small.size],
+    )
+
+
+def sum_weight_grads_plain(lefts, rights, small, width):
+    hidden = rights.shape[1] - 5 * width
+
+    def product(l_start, l_size, r_start, r_size):
+        return lax.dot_general(
+            lefts[:, l_start : l_start + l_size],
+            rights[:, r_start : r_start + r_size],
+            (((0,), (0,)), ((), ())),
+            preferred_element_type=jnp.float32,
+        )
+
+    totals = (
+        product(0, width, 0, 3 * width),
+        product(width, width, 3 * width, width),
+        product(2 * width, width, 4 * width, hidden),
+        product(3 * width, hidden, 4 * width + hidden, width),
+        jnp.pad(small, (0, -small.size % lax.axis_size("dp"))),
+    )
+    totals = lax.psum_scatter(totals, "dp", scatter_dimension=0, tiled=True)
+    whole = lax.all_gather(as_sent(totals), "dp", axis=0, tiled=True)
+    whole = jax.tree.map(lambda part: part.astype(jnp.float32), whole)
+    return whole[:4] + (whole[4][: small.size],)
 
 
 def per_device(
@@ -273,23 +606,35 @@
     layer_outputs = jnp.where(first, jnp.stack(results[:micro]), jnp.stack(results[1:]))[None]
     returned = jnp.zeros_like(inputs[0])
     grads_in = []
-    totals = None
+    lefts, rights = ([], [])
+    small_total = None
     for tick in range(micro + 1):
         index = micro - tick - section_index
         valid = (index >= 0) & (index < micro)
         own = cotangent[max(micro - 1 - tick, 0)]
         upstream = jnp.where(first, returned, own)
         upstream = jnp.where(valid, upstream, jnp.zeros_like(upstream))
-        d_in, grads = run_backward(kept_inputs[micro - tick], weights, keeps_for(index), upstream)
+        d_in, left, right, small = run_backward(
+            kept_inputs[micro - tick], weights, keeps_for(index), upstream
+        )
         grads_in.append(d_in)
         if tick < micro:
             returned = from_behind(d_in, "section", -1)
-        totals = grads if totals is None else tuple((t + s for t, s in zip(totals, grads)))
-    totals = lax.psum_scatter(totals, "dp", scatter_dimension=0, tiled=True)
-    whole = jax.tree.map(
-        lambda part, own: part.astype(own.dtype),
-        lax.all_gather(as_sent(totals), "dp", axis=0, tiled=True),
-        totals,
+        pad = -left.shape[0] % 16
+        lefts.append(jnp.pad(left, ((0, pad), (0, 0))))
+        rights.append(jnp.pad(right, ((0, pad), (0, 0))))
+        small_total = small if small_total is None else small_total + small
+    lefts = jnp.concatenate(lefts)
+    rights = jnp.concatenate(rights)
+    width = inputs.shape[-1]
+    qkv, proj, up, down, small = sum_weight_grads(lefts, rights, small_total, width)
+    hidden = up.shape[1]
+    sizes = (width, width, 2 * width, width, width, width, hidden, width)
+    starts = [sum(sizes[:i]) for i in range(len(sizes))]
+    parts = [small[s : s + size] for s, size in zip(starts, sizes)]
+    whole = (
+        parts[0], parts[1], qkv, parts[2], proj, parts[3],
+        parts[4], parts[5], up, parts[6], down, parts[7],
     )
     input_grads = jnp.where(
         first, jnp.stack(grads_in[1:][::-1]), jnp.stack(grads_in[:micro][::-1])

time: 951 us -> 767 us (0.81)
  waiting for transfers between devices: 310 us -> 14.2 us
  Pallas kernels: 0 us -> 233 us
  blocking collectives: 118 us -> 0 us
  matrix products: 294 us -> 203 us
  local copies, waits for them, and re-layouts: 92.6 us -> 178 us
  other arithmetic: 76.9 us -> 97.4 us
  between operations: 22 us -> 4.14 us
    reduce_scatter x4 -> x0, waiting for transfers between devices: 272 us -> none  [per_device(): totals = lax.psum_scatter(totals, 'dp', scatter_dimension=0, tiled=True)]
    pallas_call x0 -> x1, Pallas kernels: none -> 233 us  [sum_weight_grads(): pl.pallas_call(functools.partial(reduce_kernel, count, width, hidden), ou...]
    dot_general x20 -> x0, matrix products: 125 us -> none  [the longest x5 47.7 us: run_backward(): grad_down = jnp.dot(g_low.T, d_mlp, preferred_element_type=jnp.float32)]
    unnamed x2 -> x0, blocking collectives: 118 us -> none
    unnamed x663 -> x606, local copies, waits for them, and re-layouts: 32.1 us -> 75.9 us
    reshape x0 -> x21, local copies, waits for them, and re-layouts: none -> 39.8 us  [the longest x5 9.41 us: run_forward(): attended_low = attended.astype(jnp.bfloat16).reshape(rows, width)]
    broadcast_in_dim x5 -> x0, other arithmetic: 23.8 us -> none  [the longest x1 7.42 us: per_device(): whole[8][None]]
    all_gather x4 -> x0, waiting for transfers between devices: 16.1 us -> none  [per_device(): lax.all_gather(as_sent(totals), 'dp', axis=0, tiled=True)]
  transfers between devices with their start and end apart: 16 -> 8, of which waited for: 11 -> 3; matrix products, arithmetic and copies ran while one was open for 22% -> 7% of each run, Pallas kernels for 0% -> 0%
where the time goes in v1:
time: 767 us; the launch traced here: 754 us
  Pallas kernels  233 us (30%)
  matrix products  203 us (26%)
  local copies, waits for them, and re-layouts  178 us (23%)
  other arithmetic  97.4 us (13%)
  starting transfers between devices  24 us (3%)
  waiting for transfers between devices  14.2 us (2%)
    pallas_call x1, Pallas kernels, sum_weight_grads(): pl.pallas_call(functools.partial(reduce_kernel, count, width, hidden), ou...  233 us
    unnamed x606, local copies, waits for them, and re-layouts  75.9 us
    dot_general x5, matrix products, run_forward(): u_val = jnp.dot(c_low, w_up, preferred_element_type=jnp.float32) + b_up  44.8 us
    dot_general x5, matrix products, run_backward(): d_gel = jnp.dot(d_mlp, w_down.T, preferred_element_type=jnp.float32)  25.2 us
    ppermute x8, starting transfers between devices, from_behind(): lax.ppermute(value, axis, [(source, source + steps) for source in range(i...  24 us
    dot_general x5, matrix products, run_backward(): d_a = jnp.dot(d_qkv, w_qkv.T, preferred_element_type=jnp.float32)  21.6 us
    sub x5, matrix products, run_forward(): expd = jnp.exp(scores - top)  20.8 us
    unnamed x26, other arithmetic  16.4 us
  transfers between devices with their start and end apart: 8, of which 3 were waited for; matrix products, arithmetic and copies ran while one was open for 7% of the time, Pallas kernels for 0%

profile of v1, /device:TPU:1, one launch (start us, length us, event | category | flops | bytes accessed | tf_op | source)
XLA Modules:
  0.0 754.3 jit_solution(16169863624916975367)
XLA Ops:
  9.4 5.6 fusion.562
  23.8 4.2 fusion.564
  27.9 2.2 convolution_convert_fusion.9
  32.9 9.4 %fusion.132 = (bf16[198,3072]{1,0:T(8,128)(2,1)S(1)}, f32[198,3072]{1,0:T(8,128)}) fusion(f32[3072]{0:T(1024)S(1)} %bitcast.926, bf16[198,768]{1,0:T(8,128)(2,1)S(1)} %add_convert_fusion.4, bf16[1,768,3072]{2,1,0:T(8,128)(2,1)} %param.24), kind=kOutput, calls=%fused_computation.120 | convolution fusion | flops 974426112 | bytes 8684544 | tf_op jit(solution)/shard_map/dot_general | solution.py:104
  44.3 4.3 collective-permute-start
  48.5 5.6 collective-permute-done
  63.0 4.2 fusion.566
  72.0 8.8 %fusion.135 = (bf16[198,3072]{1,0:T(8,128)(2,1)S(1)}, f32[198,3072]{1,0:T(8,128)}) fusion(f32[3072]{0:T(1024)S(1)} %bitcast.927, bf16[198,768]{1,0:T(8,128)(2,1)S(1)} %add_convert_fusion.3, bf16[1,768,3072]{2,1,0:T(8,128)(2,1)} %param.24), kind=kOutput, calls=%fused_computation.123 | convolution fusion | flops 974426112 | bytes 8684544 | tf_op jit(solution)/shard_map/dot_general | solution.py:104
  82.9 4.7 collective-permute-start.1
  87.6 4.5 collective-permute-done.1
  100.9 4.1 fusion.568
  109.9 8.8 %fusion.138 = (bf16[198,3072]{1,0:T(8,128)(2,1)S(1)}, f32[198,3072]{1,0:T(8,128)}) fusion(f32[3072]{0:T(1024)S(1)} %bitcast.928, bf16[198,768]{1,0:T(8,128)(2,1)S(1)} %add_convert_fusion.2, bf16[1,768,3072]{2,1,0:T(8,128)(2,1)} %param.24), kind=kOutput, calls=%fused_computation.126 | convolution fusion | flops 974426112 | bytes 8684544 | tf_op jit(solution)/shard_map/dot_general | solution.py:104
  120.7 4.3 collective-permute-start.2
  125.0 4.1 collective-permute-done.2
  137.8 4.2 fusion.570
  142.0 2.2 convolution_convert_fusion.6
  147.0 8.8 %fusion.141 = (bf16[198,3072]{1,0:T(8,128)(2,1)S(1)}, f32[198,3072]{1,0:T(8,128)}) fusion(f32[3072]{0:T(1024)S(1)} %bitcast.929, bf16[198,768]{1,0:T(8,128)(2,1)S(1)} %add_convert_fusion.1, bf16[1,768,3072]{2,1,0:T(8,128)(2,1)} %param.24), kind=kOutput, calls=%fused_computation.129 | convolution fusion | flops 974426112 | bytes 8684544 | tf_op jit(solution)/shard_map/dot_general | solution.py:104
  155.9 2.6 fusion.314
  158.6 5.1 collective-permute-start.3
  163.6 2.9 fusion.561
  168.4 3.1 convert_reduce_fusion.23
  187.7 4.2 fusion.572
  191.9 2.9 convolution_convert_fusion.5
  196.7 2.6 fusion.573
  199.8 8.9 %fusion.144 = (bf16[198,3072]{1,0:T(8,128)(2,1)}, f32[198,3072]{1,0:T(8,128)S(1)}) fusion(f32[3072]{0:T(1024)S(1)} %bitcast.930, bf16[198,768]{1,0:T(8,128)(2,1)S(1)} %add_convert_fusion, bf16[1,768,3072]{2,1,0:T(8,128)(2,1)} %param.24), kind=kOutput, calls=%fused_computation.132 | convolution fusion | flops 974426112 | bytes 8684544 | tf_op jit(solution)/shard_map/dot_general | solution.py:104
  208.7 5.4 convert_reduce_fusion.4
  214.1 5.2 multiply_reduce_fusion.14
  219.3 2.5 convert_reduce_fusion.24
  225.7 3.2 convolution_convert_fusion.4
  236.7 2.2 convert_reduce_fusion.9
  238.9 4.3 fusion.421
  259.5 2.6 fusion.203
  262.2 5.4 fusion.320
  269.0 3.5 convert_reduce_fusion.3
  272.5 2.4 multiply_reduce_fusion.13
  275.0 2.4 convert_reduce_fusion.22
  281.3 3.2 convolution_convert_fusion.3
  292.2 2.2 convert_reduce_fusion.8
  294.4 4.3 fusion.412
  317.5 2.3 fusion.207
  325.1 5.4 convert_reduce_fusion.2
  330.6 2.4 multiply_reduce_fusion.12
  333.0 2.4 convert_reduce_fusion.20
  339.2 3.2 convolution_convert_fusion.2
  352.3 4.3 fusion.403
  372.7 2.3 fusion.211
  376.6 5.5 convert_reduce_fusion.1
  382.1 2.4 multiply_reduce_fusion.11
  384.5 2.4 convert_reduce_fusion.18
  390.8 3.2 convolution_convert_fusion.1
  401.7 2.2 convert_reduce_fusion.6
  403.9 4.3 fusion.394
  427.0 2.6 fusion.215
  434.3 5.4 convert_reduce_fusion
  439.8 2.4 multiply_reduce_fusion.10
  442.2 2.4 convert_reduce_fusion.16
  448.5 3.2 convolution_convert_fusion
  459.4 2.2 convert_reduce_fusion.5
  461.6 4.3 fusion.385
  481.4 2.2 reshape.1375.small_ref
  493.1 233.4 %shard_map.254 = (bf16[16,48,2304]{2,1,0:T(8,128)(2,1)}, bf16[16,48,768]{2,1,0:T(8,128)(2,1)}, bf16[16,48,3072]{2,1,0:T(8,128)(2,1)}, bf16[4,16,48,768]{3,2,1,0:T(8,128)(2,1)}, bf16[16,48,256]{2,1,0:T(8,128)(2,1)}) custom-call(bf16[1040,5376]{1,0:T(8,128)(2,1)} %fusion.219.left_ref, bf16[1040,6912]{1,0:T(8,128)(2,1)} %pad_dynamic-update-slice_fusion.right_ref, ...), custom_call_target="tpu_custom_call" | custom-call | tf_op jit(solution)/shard_map/pallas_call | solution.py:478
  740.1 3.9 bitcast_convert_fusion.1
  744.6 5.0 bitcast_convert_fusion
  749.7 4.5 convert.134
  (824 shorter events, 265.2 us)
Async XLA Ops:
  0.6 14.7 %copy-start = (bf16[1,768,2304]{2,1,0:T(8,128)(2,1)S(1)}, bf16[1,768,2304]{2,1,0:T(8,128)(2,1)}, u32[]{:S(2)}) copy-start(bf16[1,768,2304]{2,1,0:T(8,128)(2,1)} %param.18) | copy-start | bytes 10616836
  32.1 10.3 %copy-start.10 = (f32[198,768]{1,0:T(8,128)}, f32[198,768]{1,0:T(8,128)S(1)}, u32[]{:S(2)}) copy-start(f32[198,768]{1,0:T(8,128)S(1)} %get-tuple-element.171) | copy-start | bytes 1824772
  32.1 10.2 %slice-start.4 = ((s8[4718592]{0:T(1024)(128)(4,1)}), s8[4194304]{0:T(1024)(128)(4,1)S(1)}, s32[]{:S(2)}) async-start(s8[4718592]{0:T(1024)(128)(4,1)} %bitcast.908), calls=%async_computation.4 | async-start | bytes 8388608
  32.9 9.4 %copy-start.78 = (bf16[198,768]{1,0:T(8,128)(2,1)}, bf16[198,768]{1,0:T(8,128)(2,1)S(1)}, u32[]{:S(2)}) copy-start(bf16[198,768]{1,0:T(8,128)(2,1)S(1)} %add_convert_fusion.4) | copy-start | bytes 912388
  32.9 9.4 %copy-start.229 = (f32[768]{0:T(1024)S(1)}, f32[768]{0:T(1024)}, u32[]{:S(2)}) copy-start(f32[768]{0:T(1024)} %reduce.42) | copy-start | bytes 9220
  32.9 9.5 %slice-start.5 = ((s8[4718592]{0:T(1024)(128)(4,1)}), s8[524288]{0:T(1024)(128)(4,1)S(1)}, s32[]{:S(2)}) async-start(s8[4718592]{0:T(1024)(128)(4,1)} %bitcast.908), calls=%async_computation.5 | async-start | bytes 1048576
  42.4 11.8 %copy-start.63 = (bf16[1,1,198,768]{3,0,2,1:T(2,128)(2,1)S(1)}, bf16[1,1,198,768]{3,0,2,1:T(2,128)(2,1)}, u32[]{:S(2)}) copy-start(bf16[1,1,198,768]{3,0,2,1:T(2,128)(2,1)} %get-tuple-element.145) | copy-start | bytes 912388
  42.4 12.2 %copy-start.153 = (f32[768]{0:T(1024)S(1)}, f32[768]{0:T(1024)}, u32[]{:S(2)}) copy-start(f32[768]{0:T(1024)} %reduce.36) | copy-start | bytes 9220
  44.3 11.4 %copy-start.145 = (bf16[198,768]{1,0:T(8,128)(2,1)}, bf16[198,768]{1,0:T(8,128)(2,1)S(1)}, u32[]{:S(2)}) copy-start(bf16[198,768]{1,0:T(8,128)(2,1)S(1)} %fusion.305) | copy-start | bytes 912388
  44.3 9.9 %collective-permute-start = (bf16[1,198,768]{2,1,0:T(8,128)(2,1)S(1)}, bf16[1,198,768]{2,1,0:T(8,128)(2,1)S(1)}, u32[]{:S(2)}, u32[]{:S(2)}) collective-permute-start(bf16[1,198,768]{2,1,0:T(8,128)(2,1)S(1)} %bitcast.901), channel_id=1, source_target_pairs={{0,16},{1,17},{2,18},{3,19},{4,20},{5,21},{6,22},{7,23},{8,24},{9,... | collective-permute-start | bytes 912392 | tf_op jit(solution)/shard_map/ppermute | solution.py:21
  69.4 11.5 %slice-start.6 = ((s8[4718592]{0:T(1024)(128)(4,1)}), s8[4194304]{0:T(1024)(128)(4,1)S(1)}, s32[]{:S(2)}) async-start(s8[4718592]{0:T(1024)(128)(4,1)} %bitcast.910), calls=%async_computation.6 | async-start | bytes 8388608
  70.7 10.2 %copy-start.12 = (f32[198,768]{1,0:T(8,128)}, f32[198,768]{1,0:T(8,128)S(1)}, u32[]{:S(2)}) copy-start(f32[198,768]{1,0:T(8,128)S(1)} %get-tuple-element.177) | copy-start | bytes 1824772
  72.0 8.9 %copy-start.80 = (bf16[198,768]{1,0:T(8,128)(2,1)}, bf16[198,768]{1,0:T(8,128)(2,1)S(1)}, u32[]{:S(2)}) copy-start(bf16[198,768]{1,0:T(8,128)(2,1)S(1)} %add_convert_fusion.3) | copy-start | bytes 912388
  72.0 8.9 %copy-start.230 = (f32[768]{0:T(1024)S(1)}, f32[768]{0:T(1024)}, u32[]{:S(2)}) copy-start(f32[768]{0:T(1024)} %reduce.42) | copy-start | bytes 9220
  72.0 8.9 %slice-start.7 = ((s8[4718592]{0:T(1024)(128)(4,1)}), s8[524288]{0:T(1024)(128)(4,1)S(1)}, s32[]{:S(2)}) async-start(s8[4718592]{0:T(1024)(128)(4,1)} %bitcast.910), calls=%async_computation.7 | async-start | bytes 1048576
  80.9 11.2 %copy-start.62 = (bf16[1,1,198,768]{3,0,2,1:T(2,128)(2,1)S(1)}, bf16[1,1,198,768]{3,0,2,1:T(2,128)(2,1)}, u32[]{:S(2)}) copy-start(bf16[1,1,198,768]{3,0,2,1:T(2,128)(2,1)} %get-tuple-element.144) | copy-start | bytes 912388
  80.9 11.6 %copy-start.154 = (f32[768]{0:T(1024)S(1)}, f32[768]{0:T(1024)}, u32[]{:S(2)}) copy-start(f32[768]{0:T(1024)} %reduce.36) | copy-start | bytes 9220
  82.9 10.7 %copy-start.147 = (bf16[198,768]{1,0:T(8,128)(2,1)}, bf16[198,768]{1,0:T(8,128)(2,1)S(1)}, u32[]{:S(2)}) copy-start(bf16[198,768]{1,0:T(8,128)(2,1)S(1)} %fusion.308) | copy-start | bytes 912388
  82.9 9.2 %collective-permute-start.1 = (bf16[1,198,768]{2,1,0:T(8,128)(2,1)S(1)}, bf16[1,198,768]{2,1,0:T(8,128)(2,1)S(1)}, u32[]{:S(2)}, u32[]{:S(2)}) collective-permute-start(bf16[1,198,768]{2,1,0:T(8,128)(2,1)S(1)} %bitcast.903), channel_id=1, source_target_pairs={{0,16},{1,17},{2,18},{3,19},{4,20},{5,21},{6,22},{7,23},{8,24},{9,... | collective-permute-start | bytes 912392 | tf_op jit(solution)/shard_map/ppermute | solution.py:21
  107.3 11.4 %slice-start.8 = ((s8[4718592]{0:T(1024)(128)(4,1)}), s8[4194304]{0:T(1024)(128)(4,1)S(1)}, s32[]{:S(2)}) async-start(s8[4718592]{0:T(1024)(128)(4,1)} %bitcast.912), calls=%async_computation.8 | async-start | bytes 8388608
  108.6 10.1 %copy-start.14 = (f32[198,768]{1,0:T(8,128)}, f32[198,768]{1,0:T(8,128)S(1)}, u32[]{:S(2)}) copy-start(f32[198,768]{1,0:T(8,128)S(1)} %get-tuple-element.183) | copy-start | bytes 1824772
  118.8 10.3 %copy-start.32 = (bf16[1,1,198,768]{3,0,2,1:T(2,128)(2,1)S(1)}, bf16[1,1,198,768]{3,0,2,1:T(2,128)(2,1)}, u32[]{:S(2)}) copy-start(bf16[1,1,198,768]{3,0,2,1:T(2,128)(2,1)} %get-tuple-element.143) | copy-start | bytes 912388
  118.8 10.7 %copy-start.155 = (f32[768]{0:T(1024)S(1)}, f32[768]{0:T(1024)}, u32[]{:S(2)}) copy-start(f32[768]{0:T(1024)} %reduce.36) | copy-start | bytes 9220
  120.7 9.8 %copy-start.149 = (bf16[198,768]{1,0:T(8,128)(2,1)}, bf16[198,768]{1,0:T(8,128)(2,1)S(1)}, u32[]{:S(2)}) copy-start(bf16[198,768]{1,0:T(8,128)(2,1)S(1)} %fusion.311) | copy-start | bytes 912388
  120.7 8.4 %collective-permute-start.2 = (bf16[1,198,768]{2,1,0:T(8,128)(2,1)S(1)}, bf16[1,198,768]{2,1,0:T(8,128)(2,1)S(1)}, u32[]{:S(2)}, u32[]{:S(2)}) collective-permute-start(bf16[1,198,768]{2,1,0:T(8,128)(2,1)S(1)} %bitcast.905), channel_id=1, source_target_pairs={{0,16},{1,17},{2,18},{3,19},{4,20},{5,21},{6,22},{7,23},{8,24},{9,... | collective-permute-start | bytes 912392 | tf_op jit(solution)/shard_map/ppermute | solution.py:21
  144.3 11.6 %slice-start.10 = ((s8[4718592]{0:T(1024)(128)(4,1)}), s8[4194304]{0:T(1024)(128)(4,1)S(1)}, s32[]{:S(2)}) async-start(s8[4718592]{0:T(1024)(128)(4,1)} %bitcast.914), calls=%async_computation.10 | async-start | bytes 8388608
  145.7 10.2 %copy-start.16 = (f32[198,768]{1,0:T(8,128)}, f32[198,768]{1,0:T(8,128)S(1)}, u32[]{:S(2)}) copy-start(f32[198,768]{1,0:T(8,128)S(1)} %get-tuple-element.189) | copy-start | bytes 1824772
  147.0 8.9 %copy-start.232 = (f32[768]{0:T(1024)S(1)}, f32[768]{0:T(1024)}, u32[]{:S(2)}) copy-start(f32[768]{0:T(1024)} %reduce.42) | copy-start | bytes 9220
  147.0 8.9 %slice-start.11 = ((s8[4718592]{0:T(1024)(128)(4,1)}), s8[524288]{0:T(1024)(128)(4,1)S(1)}, s32[]{:S(2)}) async-start(s8[4718592]{0:T(1024)(128)(4,1)} %bitcast.914), calls=%async_computation.11 | async-start | bytes 1048576
  158.6 18.6 %collective-permute-start.3 = (bf16[1,198,768]{2,1,0:T(8,128)(2,1)}, bf16[1,198,768]{2,1,0:T(8,128)(2,1)}, u32[]{:S(2)}, u32[]{:S(2)}) collective-permute-start(bf16[1,198,768]{2,1,0:T(8,128)(2,1)} %bitcast.55), channel_id=1, source_target_pairs={{0,16},{1,17},{2,18},{3,19},{4,20},{5,21},{6,22},{7,23},{8,24},{9,... | collective-permute-start | bytes 912392 | tf_op jit(solution)/shard_map/ppermute | solution.py:21
  199.3 20.0 %copy-start.18 = (f32[198,768]{1,0:T(8,128)}, f32[198,768]{1,0:T(8,128)S(1)}, u32[]{:S(2)}) copy-start(f32[198,768]{1,0:T(8,128)S(1)} %get-tuple-element.195) | copy-start | bytes 1824772
  199.8 8.9 %copy-start.86 = (bf16[198,768]{1,0:T(8,128)(2,1)}, bf16[198,768]{1,0:T(8,128)(2,1)S(1)}, u32[]{:S(2)}) copy-start(bf16[198,768]{1,0:T(8,128)(2,1)S(1)} %add_convert_fusion) | copy-start | bytes 912388
  199.8 8.9 %copy-start.52 = (bf16[1,1,198,768]{3,2,1,0:T(8,128)(2,1)S(1)}, bf16[1,1,198,768]{3,2,1,0:T(8,128)(2,1)}, u32[]{:S(2)}) copy-start(bf16[1,1,198,768]{3,2,1,0:T(8,128)(2,1)} %get-tuple-element.100) | copy-start | bytes 912388
  245.0 10.9 %copy-start.116 = (bf16[198,768]{1,0:T(8,128)(2,1)S(1)}, bf16[198,768]{1,0:T(8,128)(2,1)}, u32[]{:S(2)}) copy-start(bf16[198,768]{1,0:T(8,128)(2,1)} %copy.173) | copy-start | bytes 912388
  245.1 11.0 %copy-start.112 = (bf16[198,768]{1,0:T(8,128)(2,1)S(1)}, bf16[198,768]{1,0:T(8,128)(2,1)}, u32[]{:S(2)}) copy-start(bf16[198,768]{1,0:T(8,128)(2,1)} %copy.174) | copy-start | bytes 912388
  245.1 11.0 %copy-start.51 = (bf16[198,768]{1,0:T(8,128)(2,1)S(1)}, bf16[198,768]{1,0:T(8,128)(2,1)}, u32[]{:S(2)}) copy-start(bf16[198,768]{1,0:T(8,128)(2,1)} %copy-done.50) | copy-start | bytes 912388
  245.1 11.1 %copy-start.111 = (bf16[198,3072]{1,0:T(8,128)(2,1)S(1)}, bf16[198,3072]{1,0:T(8,128)(2,1)}, u32[]{:S(2)}) copy-start(bf16[198,3072]{1,0:T(8,128)(2,1)} %copy-done.110) | copy-start | bytes 3649540
  253.4 14.2 %collective-permute-start.4 = (bf16[1,198,768]{2,1,0:T(8,128)(2,1)S(1)}, bf16[1,198,768]{2,1,0:T(8,128)(2,1)S(1)}, u32[]{:S(2)}, u32[]{:S(2)}) collective-permute-start(bf16[1,198,768]{2,1,0:T(8,128)(2,1)S(1)} %bitcast.869), channel_id=1, source_target_pairs={{16,0},{17,1},{18,2},{19,3},{20,4},{21,5},{22,6},{23,7},{24,8},{25... | collective-permute-start | bytes 912392 | tf_op jit(solution)/shard_map/ppermute | solution.py:21
  254.8 14.1 %slice-start.12 = ((s8[4718592]{0:T(1024)(128)(4,1)}), s8[4194304]{0:T(1024)(128)(4,1)S(1)}, s32[]{:S(2)}) async-start(s8[4718592]{0:T(1024)(128)(4,1)} %bitcast.916), calls=%async_computation.12 | async-start | bytes 8388608
  259.5 9.4 %slice-start.13 = ((s8[4718592]{0:T(1024)(128)(4,1)}), s8[524288]{0:T(1024)(128)(4,1)S(1)}, s32[]{:S(2)}) async-start(s8[4718592]{0:T(1024)(128)(4,1)} %bitcast.916), calls=%async_computation.13 | async-start | bytes 1048576
  262.2 10.3 %slice-start.14 = ((s8[4718592]{0:T(1024)(128)(4,1)}), s8[4194304]{0:T(1024)(128)(4,1)S(1)}, s32[]{:S(2)}) async-start(s8[4718592]{0:T(1024)(128)(4,1)} %bitcast.918), calls=%async_computation.14 | async-start | bytes 8388608
  300.6 10.8 %copy-start.117 = (bf16[198,768]{1,0:T(8,128)(2,1)S(1)}, bf16[198,768]{1,0:T(8,128)(2,1)}, u32[]{:S(2)}) copy-start(bf16[198,768]{1,0:T(8,128)(2,1)} %copy.176) | copy-start | bytes 912388
  300.6 10.8 %copy-start.113 = (bf16[198,768]{1,0:T(8,128)(2,1)S(1)}, bf16[198,768]{1,0:T(8,128)(2,1)}, u32[]{:S(2)}) copy-start(bf16[198,768]{1,0:T(8,128)(2,1)} %copy.177) | copy-start | bytes 912388
  300.7 10.9 %copy-start.45 = (bf16[198,768]{1,0:T(8,128)(2,1)S(1)}, bf16[198,768]{1,0:T(8,128)(2,1)}, u32[]{:S(2)}) copy-start(bf16[198,768]{1,0:T(8,128)(2,1)} %copy-done.44) | copy-start | bytes 912388
  300.7 10.9 %copy-start.105 = (bf16[198,3072]{1,0:T(8,128)(2,1)S(1)}, bf16[198,3072]{1,0:T(8,128)(2,1)}, u32[]{:S(2)}) copy-start(bf16[198,3072]{1,0:T(8,128)(2,1)} %copy-done.104) | copy-start | bytes 3649540
  309.0 14.7 %collective-permute-start.5 = (bf16[1,198,768]{2,1,0:T(8,128)(2,1)S(1)}, bf16[1,198,768]{2,1,0:T(8,128)(2,1)S(1)}, u32[]{:S(2)}, u32[]{:S(2)}) collective-permute-start(bf16[1,198,768]{2,1,0:T(8,128)(2,1)S(1)} %bitcast.871), channel_id=1, source_target_pairs={{16,0},{17,1},{18,2},{19,3},{20,4},{21,5},{22,6},{23,7},{24,8},{25... | collective-permute-start | bytes 912392 | tf_op jit(solution)/shard_map/ppermute | solution.py:21
  315.0 10.1 %copy-start.243 = (f32[198,3072]{1,0:T(8,128)S(1)}, f32[198,3072]{1,0:T(8,128)}, u32[]{:S(2)}) copy-start(f32[198,3072]{1,0:T(8,128)} %get-tuple-element.185) | copy-start | bytes 7299076
  317.5 13.0 %slice-start.16 = ((s8[4718592]{0:T(1024)(128)(4,1)}), s8[4194304]{0:T(1024)(128)(4,1)S(1)}, s32[]{:S(2)}) async-start(s8[4718592]{0:T(1024)(128)(4,1)} %bitcast.920), calls=%async_computation.16 | async-start | bytes 8388608
  358.5 10.8 %copy-start.118 = (bf16[198,768]{1,0:T(8,128)(2,1)S(1)}, bf16[198,768]{1,0:T(8,128)(2,1)}, u32[]{:S(2)}) copy-start(bf16[198,768]{1,0:T(8,128)(2,1)} %copy.179) | copy-start | bytes 912388
  358.5 10.9 %copy-start.114 = (bf16[198,768]{1,0:T(8,128)(2,1)S(1)}, bf16[198,768]{1,0:T(8,128)(2,1)}, u32[]{:S(2)}) copy-start(bf16[198,768]{1,0:T(8,128)(2,1)} %copy.180) | copy-start | bytes 912388
  358.5 10.9 %copy-start.47 = (bf16[198,768]{1,0:T(8,128)(2,1)S(1)}, bf16[198,768]{1,0:T(8,128)(2,1)}, u32[]{:S(2)}) copy-start(bf16[198,768]{1,0:T(8,128)(2,1)} %copy-done.46) | copy-start | bytes 912388
  358.5 10.9 %copy-start.107 = (bf16[198,3072]{1,0:T(8,128)(2,1)S(1)}, bf16[198,3072]{1,0:T(8,128)(2,1)}, u32[]{:S(2)}) copy-start(bf16[198,3072]{1,0:T(8,128)(2,1)} %copy-done.106) | copy-start | bytes 3649540
  366.9 8.3 %collective-permute-start.6 = (bf16[1,198,768]{2,1,0:T(8,128)(2,1)S(1)}, bf16[1,198,768]{2,1,0:T(8,128)(2,1)S(1)}, u32[]{:S(2)}, u32[]{:S(2)}) collective-permute-start(bf16[1,198,768]{2,1,0:T(8,128)(2,1)S(1)} %bitcast.873), channel_id=1, source_target_pairs={{16,0},{17,1},{18,2},{19,3},{20,4},{21,5},{22,6},{23,7},{24,8},{25... | collective-permute-start | bytes 912392 | tf_op jit(solution)/shard_map/ppermute | solution.py:21
  372.7 9.4 %slice-start.18 = ((s8[4718592]{0:T(1024)(128)(4,1)}), s8[4194304]{0:T(1024)(128)(4,1)S(1)}, s32[]{:S(2)}) async-start(s8[4718592]{0:T(1024)(128)(4,1)} %bitcast.922), calls=%async_computation.18 | async-start | bytes 8388608
  410.1 10.8 %copy-start.119 = (bf16[198,768]{1,0:T(8,128)(2,1)S(1)}, bf16[198,768]{1,0:T(8,128)(2,1)}, u32[]{:S(2)}) copy-start(bf16[198,768]{1,0:T(8,128)(2,1)} %copy.182) | copy-start | bytes 912388
  410.1 10.8 %copy-start.115 = (bf16[198,768]{1,0:T(8,128)(2,1)S(1)}, bf16[198,768]{1,0:T(8,128)(2,1)}, u32[]{:S(2)}) copy-start(bf16[198,768]{1,0:T(8,128)(2,1)} %copy.183) | copy-start | bytes 912388
  410.1 10.9 %copy-start.49 = (bf16[198,768]{1,0:T(8,128)(2,1)S(1)}, bf16[198,768]{1,0:T(8,128)(2,1)}, u32[]{:S(2)}) copy-start(bf16[198,768]{1,0:T(8,128)(2,1)} %copy-done.48) | copy-start | bytes 912388
  410.1 10.9 %copy-start.109 = (bf16[198,3072]{1,0:T(8,128)(2,1)S(1)}, bf16[198,3072]{1,0:T(8,128)(2,1)}, u32[]{:S(2)}) copy-start(bf16[198,3072]{1,0:T(8,128)(2,1)} %copy-done.108) | copy-start | bytes 3649540
  418.5 15.0 %collective-permute-start.7 = (bf16[1,198,768]{2,1,0:T(8,128)(2,1)S(1)}, bf16[1,198,768]{2,1,0:T(8,128)(2,1)S(1)}, u32[]{:S(2)}, u32[]{:S(2)}) collective-permute-start(bf16[1,198,768]{2,1,0:T(8,128)(2,1)S(1)} %bitcast.875), channel_id=1, source_target_pairs={{16,0},{17,1},{18,2},{19,3},{20,4},{21,5},{22,6},{23,7},{24,8},{25... | collective-permute-start | bytes 912392 | tf_op jit(solution)/shard_map/ppermute | solution.py:21
  424.5 9.7 %copy-start.241 = (f32[198,3072]{1,0:T(8,128)S(1)}, f32[198,3072]{1,0:T(8,128)}, u32[]{:S(2)}) copy-start(f32[198,3072]{1,0:T(8,128)} %get-tuple-element.173) | copy-start | bytes 7299076
  427.0 12.7 %slice-start.20 = ((s8[4718592]{0:T(1024)(128)(4,1)}), s8[4194304]{0:T(1024)(128)(4,1)S(1)}, s32[]{:S(2)}) async-start(s8[4718592]{0:T(1024)(128)(4,1)} %bitcast.924), calls=%async_computation.20 | async-start | bytes 8388608
  493.1 235.8 %copy-start.235 = (f32[198]{0:T(256)S(1)}, f32[198]{0:T(256)}, u32[]{:S(2)}) copy-start(f32[198]{0:T(256)} %get-tuple-element.71) | copy-start | bytes 2380
  493.1 235.8 %copy-start.234 = (f32[198]{0:T(256)S(1)}, f32[198]{0:T(256)}, u32[]{:S(2)}) copy-start(f32[198]{0:T(256)} %get-tuple-element.72) | copy-start | bytes 2380
  493.1 235.8 %copy-start.208 = (f32[198]{0:T(256)S(1)}, f32[198]{0:T(256)}, u32[]{:S(2)}) copy-start(f32[198]{0:T(256)} %copy-done.207) | copy-start | bytes 2380
  (211 other events, 671.9 us)

commit v2 on v1

--- a/solution.py
+++ b/solution.py
@@ -15,12 +15,6 @@
 survive = 1.0 / 0.9
 
 
-def from_behind(value, axis, steps):
-    count = lax.axis_size(axis)
-    initial, last = (max(0, -steps), min(count, count - steps))
-    return lax.ppermute(value, axis, [(source, source + steps) for source in range(initial, last)])
-
-
 def as_sent(x):
 
     def short(part):
@@ -29,186 +23,410 @@
     return jax.tree.map(short, x)
 
 
-def norm_parts(values, gain, shift):
-    mean_v = jnp.mean(values, axis=-1, keepdims=True)
-    centered = values - mean_v
-    var = jnp.mean(centered * centered, axis=-1, keepdims=True)
-    factor = lax.rsqrt(var + epsilon)
-    normed = centered * factor
-    return (normed * gain + shift, normed, factor)
-
-
-def norm_back(grad_out, normed, factor, gain):
-    scaled = grad_out * gain
-    grad_in = factor * (
-        scaled
-        - jnp.mean(scaled, axis=-1, keepdims=True)
-        - normed * jnp.mean(scaled * normed, axis=-1, keepdims=True)
-    )
-    return (grad_in, jnp.sum(grad_out * normed, axis=0), jnp.sum(grad_out, axis=0))
-
-
-def gelu_slope(u):
-    return 0.5 * (1.0 + lax.erf(u / math.sqrt(2.0))) + u * jnp.exp(-0.5 * u * u) / math.sqrt(
-        2.0 * math.pi
-    )
-
-
-def run_forward(layer_in, weights, keeps):
+def meet(peer):
+    barrier = pltpu.get_barrier_semaphore()
+    pl.semaphore_signal(barrier, inc=1, device_id=peer, device_id_type=pl.DeviceIdType.MESH)
+    pl.semaphore_wait(barrier, 1)
+
+
+def norm_stats(values):
+    centered = values - jnp.mean(values, axis=-1, keepdims=True)
+    factor = lax.rsqrt(jnp.mean(centered * centered, axis=-1, keepdims=True) + epsilon)
+    return (centered * factor, factor)
+
+
+def dot_nn(a, b):
+    return lax.dot_general(a, b, (((1,), (0,)), ((), ())), preferred_element_type=jnp.float32)
+
+
+def dot_nt(a, b):
+    return lax.dot_general(a, b, (((1,), (1,)), ((), ())), preferred_element_type=jnp.float32)
+
+
+def dot_tn(a, b):
+    return lax.dot_general(a, b, (((0,), (0,)), ((), ())), preferred_element_type=jnp.float32)
+
+
+def fill_rows(dst_ref, src_ref):
+    tokens, rows = src_ref.shape[-2], dst_ref.shape[-2]
+    edge = tokens // 16 * 16
+    dst_ref[0, edge:rows, :] = jnp.zeros((rows - edge, dst_ref.shape[-1]), dst_ref.dtype)
+    dst_ref[0, 0:tokens, :] = src_ref[0, 0]
+
+
+def head_masks(rows):
+    lane = lax.broadcasted_iota(jnp.int32, (rows, 2 * HEAD_DIM), 1)
+    return (lane < HEAD_DIM, lane >= HEAD_DIM)
+
+
+def softmax_rows(query, keyed, tokens):
+    scores = dot_nt(query, keyed)
+    column = lax.broadcasted_iota(jnp.int32, scores.shape, 1)
+    scores = jnp.where(column < tokens, scores, -1e30)
+    expd = jnp.exp(scores - jnp.max(scores, axis=-1, keepdims=True))
+    return expd / jnp.sum(expd, axis=-1, keepdims=True)
+
+
+def forward_kernel(
+    keeps_ref,
+    in_ref,
+    ln1_gain,
+    ln1_bias,
+    w_qkv,
+    qv_bias,
+    w_proj,
+    b_proj,
+    ln2_gain,
+    ln2_bias,
+    w_up,
+    b_up,
+    w_down,
+    b_down,
+    y_ref,
+    held_ref,
+    left_ref,
+    qkv_ref,
+    slope_ref,
+    mid_ref,
+    recv,
+    send,
+    send_sem,
+    recv_sem,
+):
+    m = pl.program_id(0)
+    micro = pl.num_programs(0)
+    section = lax.axis_index("section")
+    peer = {"section": 1 - section}
+    tokens, width = y_ref.shape[1:]
+    hidden = w_up.shape[1]
+    rows = held_ref.shape[1]
+
+    @pl.when(m == 0)
+    def _():
+        meet(peer)
+
+    def copy_of(i):
+        return pltpu.make_async_remote_copy(
+            src_ref=send.at[i],
+            dst_ref=recv.at[i],
+            send_sem=send_sem.at[i],
+            recv_sem=recv_sem.at[i],
+            device_id=peer,
+            device_id_type=pl.DeviceIdType.MESH,
+        )
+
+    @pl.when(section == 0)
+    def _():
+        fill_rows(held_ref, in_ref)
+
+    @pl.when(section == 1)
+    def _():
+        copy_of(m).wait_recv()
+        held_ref[0] = recv[m]
+
+    h = held_ref[0].astype(jnp.float32)
+    normed, _ = norm_stats(h)
+    a_low = (normed * ln1_gain[...] + ln1_bias[...]).astype(jnp.bfloat16)
+    left_ref[0, :, 0:width] = a_low
+    for part in range(3):
+        span = slice(part * width, (part + 1) * width)
+        product = dot_nn(a_low, w_qkv[:, span])
+        if part == 0:
+            product = product + qv_bias[:, 0:width]
+        if part == 2:
+            product = product + qv_bias[:, width:]
+        qkv_ref[0, :, span] = product.astype(jnp.bfloat16)
+
+    masks = head_masks(rows)
+    pair = 2 * HEAD_DIM
+    for p in range(width // pair):
+        at = [slice(part * width + p * pair, part * width + (p + 1) * pair) for part in range(3)]
+        query, keyed, value = (qkv_ref[0, :, span] for span in at)
+        query = query * jnp.asarray(HEAD_DIM**-0.5, jnp.bfloat16)
+        joined = None
+        for mask in masks:
+            probs = softmax_rows(jnp.where(mask, query, jnp.zeros_like(query)), keyed, tokens)
+            one = dot_nn(probs.astype(jnp.bfloat16), jnp.where(mask, value, jnp.zeros_like(value)))
+            joined = one if joined is None else joined + one
+        left_ref[0, :, width + p * pair : width + (p + 1) * pair] = joined.astype(jnp.bfloat16)
+
+    branch = dot_nn(left_ref[0, :, width : 2 * width], w_proj[...]) + b_proj[...]
+    x_mid = h + keeps_ref[0, m] * branch
+    mid_ref[0] = x_mid
+    normed, _ = norm_stats(x_mid)
+    c_low = (normed * ln2_gain[...] + ln2_bias[...]).astype(jnp.bfloat16)
+    left_ref[0, :, 2 * width : 3 * width] = c_low
+    total = None
+    for part in range(hidden // width):
+        span = slice(part * width, (part + 1) * width)
+        u = dot_nn(c_low, w_up[:, span]) + b_up[:, span]
+        normal = 0.5 * (1.0 + lax.erf(u * math.sqrt(0.5)))
+        slope_ref[0, :, span] = normal + u * jnp.exp(-0.5 * u * u) * (1.0 / math.sqrt(2.0 * math.pi))
+        g_low = (u * normal).astype(jnp.bfloat16)
+        left_ref[0, :, (3 + part) * width : (4 + part) * width] = g_low
+        one = dot_nn(g_low, w_down[span, :])
+        total = one if total is None else total + one
+    y = (x_mid + keeps_ref[1, m] * (total + b_down[...])).astype(jnp.bfloat16)
+    y_ref[0] = y[0:tokens]
+
+    @pl.when(section == 0)
+    def _():
+        send[m] = y
+        copy_of(m).start()
+
+    @pl.when((section == 0) & (m == micro - 1))
+    def _():
+        for i in range(send.shape[0]):
+            copy_of(i).wait_send()
+
+
+def backward_kernel(
+    keeps_ref,
+    cot_ref,
+    held_ref,
+    qkv_ref,
+    slope_ref,
+    mid_ref,
+    ln1_gain,
+    w_qkv,
+    w_proj,
+    ln2_gain,
+    w_up,
+    w_down,
+    d_in_ref,
+    right_ref,
+    small_ref,
+    recv,
+    send,
+    upstream,
+    d_heads,
+    send_sem,
+    recv_sem,
+):
+    j = pl.program_id(0)
+    micro = pl.num_programs(0)
+    m = micro - 1 - j
+    section = lax.axis_index("section")
+    peer = {"section": 1 - section}
+    tokens, width = d_in_ref.shape[1:]
+    hidden = w_up.shape[1]
+    rows = held_ref.shape[1]
+    pair = 2 * HEAD_DIM
+    scale = HEAD_DIM**-0.5
+
+    @pl.when(j == 0)
+    def _():
+        meet(peer)
+        small_ref[...] = jnp.zeros_like(small_ref)
+
+    def copy_of(i):
+        return pltpu.make_async_remote_copy(
+            src_ref=send.at[i],
+            dst_ref=recv.at[i],
+            send_sem=send_sem.at[i],
+            recv_sem=recv_sem.at[i],
+            device_id=peer,
+            device_id_type=pl.DeviceIdType.MESH,
+        )
+
+    @pl.when(section == 1)
+    def _():
+        fill_rows(upstream, cot_ref)
+
+    @pl.when(section == 0)
+    def _():
+        copy_of(j).wait_recv()
+        upstream[0] = recv[j]
+
+    def add_small(row, values):
+        small_ref[row : row + 1, :] += jnp.sum(values, axis=0, keepdims=True)
+
+    keep_attn, keep_mlp = (keeps_ref[0, m], keeps_ref[1, m])
+    d_end = upstream[0].astype(jnp.float32)
+    dm_low = (d_end * keep_mlp).astype(jnp.bfloat16)
+    first_up = 4 * width
+    right_ref[0, :, first_up + hidden : first_up + hidden + width] = dm_low
+    parts = hidden // width
+    add_small(7 + parts, dm_low.astype(jnp.float32))
+    d_c = None
+    for part in range(parts):
+        span = slice(part * width, (part + 1) * width)
+        d_gel = dot_nt(dm_low, w_down[span, :])
+        du_low = (d_gel * slope_ref[0, :, span]).astype(jnp.bfloat16)
+        right_ref[0, :, first_up + part * width : first_up + (part + 1) * width] = du_low
+        add_small(7 + part, du_low.astype(jnp.float32))
+        one = dot_nt(du_low, w_up[:, span])
+        d_c = one if d_c is None else d_c + one
+
+    def norm_grad(grad, normed, factor, gain, row):
+        add_small(row, grad * normed)
+        add_small(row + 1, grad)
+        scaled = grad * gain
+        return factor * (
+            scaled
+            - jnp.mean(scaled, axis=-1, keepdims=True)
+            - normed * jnp.mean(scaled * normed, axis=-1, keepdims=True)
+        )
+
+    normed, factor = norm_stats(mid_ref[0])
+    d_mid = d_end + norm_grad(d_c, normed, factor, ln2_gain[...], 5)
+    dz_low = (d_mid * keep_attn).astype(jnp.bfloat16)
+    right_ref[0, :, 3 * width : first_up] = dz_low
+    add_small(4, dz_low.astype(jnp.float32))
+    d_heads[...] = dot_nt(dz_low, w_proj[...]).astype(jnp.bfloat16)
+
+    masks = head_masks(rows)
+    for p in range(width // pair):
+        at = [slice(part * width + p * pair, part * width + (p + 1) * pair) for part in range(3)]
+        query, keyed, value = (qkv_ref[0, :, span] for span in at)
+        d_out = d_heads[:, at[0]]
+        grads = [None, None, None]
+        for mask in masks:
+
+            def only(x):
+                return jnp.where(mask, x, jnp.zeros_like(x))
+
+            query_one, d_one = only(query), only(d_out)
+            probs = softmax_rows(query_one * jnp.asarray(scale, jnp.bfloat16), keyed, tokens)
+            d_probs = dot_nt(d_one, value)
+            inner = jnp.sum(d_probs * probs, axis=-1, keepdims=True)
+            ds_low = (probs * (d_probs - inner)).astype(jnp.bfloat16)
+            found = (
+                dot_nn(ds_low, only(keyed)),
+                dot_tn(ds_low, query_one),
+                dot_tn(probs.astype(jnp.bfloat16), d_one),
+            )
+            grads = [f if g is None else g + f for g, f in zip(grads, found)]
+        right_ref[0, :, at[0]] = (grads[0] * scale).astype(jnp.bfloat16)
+        right_ref[0, :, at[1]] = (grads[1] * scale).astype(jnp.bfloat16)
+        right_ref[0, :, at[2]] = grads[2].astype(jnp.bfloat16)
+
+    add_small(2, right_ref[0, :, 0:width].astype(jnp.float32))
+    add_small(3, right_ref[0, :, 2 * width : 3 * width].astype(jnp.float32))
+    d_a = dot_nt(right_ref[0, :, 0 : 3 * width], w_qkv[...])
+    normed, factor = norm_stats(held_ref[0].astype(jnp.float32))
+    d_in = d_mid + norm_grad(d_a, normed, factor, ln1_gain[...], 0)
+    d_low = d_in.astype(jnp.bfloat16)
+    d_in_ref[0] = d_low[0:tokens]
+
+    @pl.when(section == 1)
+    def _():
+        send[j] = d_low
+        copy_of(j).start()
+
+    @pl.when((section == 1) & (j == micro - 1))
+    def _():
+        for i in range(send.shape[0]):
+            copy_of(i).wait_send()
+
+
+def run_layers(inputs, cotangent, weights, keeps):
     (
-        gain_one,
-        shift_one,
-        w_qkv,
-        bias_qv,
-        w_proj,
-        b_proj,
-        gain_two,
-        shift_two,
-        w_up,
-        b_up,
-        w_down,
-        b_down,
-    ) = weights
-    images, length, width = layer_in.shape
-    heads = width // HEAD_DIM
-    rows = images * length
-    scale = HEAD_DIM ** (-0.5)
-    keep_attn = jnp.repeat(keeps[0], length)[:, None]
-    keep_mlp = jnp.repeat(keeps[1], length)[:, None]
-    h_rows = layer_in.astype(jnp.float32).reshape(rows, width)
-    a_val, normed_one, factor_one = norm_parts(h_rows, gain_one, shift_one)
-    a_low = a_val.astype(jnp.bfloat16)
-    qkv = jnp.dot(a_low, w_qkv, preferred_element_type=jnp.float32)
-    query = (
-        (qkv[:, :width] + bias_qv[:width])
-        .astype(jnp.bfloat16)
-        .reshape(images, length, heads, HEAD_DIM)
-    )
-    keyed = qkv[:, width : 2 * width].astype(jnp.bfloat16).reshape(images, length, heads, HEAD_DIM)
-    value = (
-        (qkv[:, 2 * width :] + bias_qv[width:])
-        .astype(jnp.bfloat16)
-        .reshape(images, length, heads, HEAD_DIM)
-    )
-    scores = jnp.einsum("ishd,ithd->ihst", query, keyed, preferred_element_type=jnp.float32) * scale
-    top = jnp.max(scores, axis=-1, keepdims=True)
-    expd = jnp.exp(scores - top)
-    probs = expd / jnp.sum(expd, axis=-1, keepdims=True)
-    probs_low = probs.astype(jnp.bfloat16)
-    attended = jnp.einsum("ihst,ithd->ishd", probs_low, value, preferred_element_type=jnp.float32)
-    attended_low = attended.astype(jnp.bfloat16).reshape(rows, width)
-    branch = jnp.dot(attended_low, w_proj, preferred_element_type=jnp.float32) + b_proj
-    x_mid = h_rows + keep_attn * branch
-    c_val, normed_two, factor_two = norm_parts(x_mid, gain_two, shift_two)
-    c_low = c_val.astype(jnp.bfloat16)
-    u_val = jnp.dot(c_low, w_up, preferred_element_type=jnp.float32) + b_up
-    g_low = jax.nn.gelu(u_val, approximate=False).astype(jnp.bfloat16)
-    mlp_out = jnp.dot(g_low, w_down, preferred_element_type=jnp.float32) + b_down
-    x_end = x_mid + keep_mlp * mlp_out
-    result = x_end.astype(jnp.bfloat16).reshape(images, length, width)
-    saved = (
-        normed_one,
-        factor_one,
-        a_low,
-        query,
-        keyed,
-        value,
-        probs,
-        probs_low,
-        attended_low,
-        normed_two,
-        factor_two,
-        c_low,
-        u_val,
-        g_low,
-        keep_attn,
-        keep_mlp,
-    )
-    return (result, saved)
-
-
-def run_backward(layer_in, weights, keeps, upstream):
-    (
-        gain_one,
-        shift_one,
-        w_qkv,
-        bias_qv,
-        w_proj,
-        b_proj,
-        gain_two,
-        shift_two,
-        w_up,
-        b_up,
-        w_down,
-        b_down,
-    ) = weights
-    images, length, width = layer_in.shape
-    heads = width // HEAD_DIM
-    rows = images * length
-    scale = HEAD_DIM ** (-0.5)
-    (
-        normed_one,
-        factor_one,
-        a_low,
-        query,
-        keyed,
-        value,
-        probs,
-        probs_low,
-        attended_low,
-        normed_two,
-        factor_two,
-        c_low,
-        u_val,
-        g_low,
-        keep_attn,
-        keep_mlp,
-    ) = run_forward(layer_in, weights, keeps)[1]
-    d_end = upstream.astype(jnp.float32).reshape(rows, width)
-    d_mlp = (d_end * keep_mlp).astype(jnp.bfloat16)
-    grad_down_bias = jnp.sum(d_mlp.astype(jnp.float32), axis=0)
-    d_gel = jnp.dot(d_mlp, w_down.T, preferred_element_type=jnp.float32)
-    d_up = (d_gel * gelu_slope(u_val)).astype(jnp.bfloat16)
-    grad_up_bias = jnp.sum(d_up.astype(jnp.float32), axis=0)
-    d_c = jnp.dot(d_up, w_up.T, preferred_element_type=jnp.float32)
-    d_mid_norm, grad_gain_two, grad_shift_two = norm_back(d_c, normed_two, factor_two, gain_two)
-    d_mid = d_end + d_mid_norm
-    d_branch = (d_mid * keep_attn).astype(jnp.bfloat16)
-    grad_proj_bias = jnp.sum(d_branch.astype(jnp.float32), axis=0)
-    d_att = jnp.dot(d_branch, w_proj.T, preferred_element_type=jnp.float32)
-    d_att = d_att.astype(jnp.bfloat16).reshape(images, length, heads, HEAD_DIM)
-    d_probs = jnp.einsum("ishd,ithd->ihst", d_att, value, preferred_element_type=jnp.float32)
-    d_value = jnp.einsum("ihst,ishd->ithd", probs_low, d_att, preferred_element_type=jnp.float32)
-    d_scores = probs * (d_probs - jnp.sum(d_probs * probs, axis=-1, keepdims=True))
-    d_scores = d_scores.astype(jnp.bfloat16)
-    d_query = (
-        jnp.einsum("ihst,ithd->ishd", d_scores, keyed, preferred_element_type=jnp.float32) * scale
-    )
-    d_keyed = (
-        jnp.einsum("ihst,ishd->ithd", d_scores, query, preferred_element_type=jnp.float32) * scale
-    )
-    d_qkv = jnp.concatenate(
-        [d_query.reshape(rows, width), d_keyed.reshape(rows, width), d_value.reshape(rows, width)],
-        axis=1,
-    ).astype(jnp.bfloat16)
-    column_sums = jnp.sum(d_qkv.astype(jnp.float32), axis=0)
-    grad_bias_qv = jnp.concatenate([column_sums[:width], column_sums[2 * width :]])
-    d_a = jnp.dot(d_qkv, w_qkv.T, preferred_element_type=jnp.float32)
-    d_in_norm, grad_gain_one, grad_shift_one = norm_back(d_a, normed_one, factor_one, gain_one)
-    d_in = (d_mid + d_in_norm).astype(jnp.bfloat16).reshape(images, length, width)
-    small = (
-        grad_gain_one,
-        grad_shift_one,
-        grad_bias_qv,
-        grad_proj_bias,
-        grad_gain_two,
-        grad_shift_two,
-        grad_up_bias,
-        grad_down_bias,
-    )
-    left = jnp.concatenate([a_low, attended_low, c_low, g_low], axis=1)
-    right = jnp.concatenate([d_qkv, d_branch, d_up, d_mlp], axis=1)
-    return (d_in, left, right, jnp.concatenate(small))
+        gain_one, shift_one, w_qkv, bias_qv, w_proj, b_proj,
+        gain_two, shift_two, w_up, b_up, w_down, b_down,
+    ) = (w.reshape(1, -1) if w.ndim == 1 else w for w in weights)
+    micro, _, tokens, width = inputs.shape
+    hidden = w_up.shape[1]
+    rows = tokens + -tokens % 16
+    low, dma = (jnp.bfloat16, pltpu.SemaphoreType.DMA)
+
+    def fixed(x):
+        return pl.BlockSpec(x.shape, lambda i: (0,) * x.ndim, pipeline_mode=pl.Buffered(1))
+
+    def per_step(order, *dims):
+        return pl.BlockSpec((1,) + dims, lambda i: (order(i),) + (0,) * len(dims))
+
+    def ahead(i):
+        return i
+
+    def back(i):
+        return micro - 1 - i
+
+    def params(which):
+        return pltpu.CompilerParams(
+            collective_id=which,
+            has_side_effects=True,
+            dimension_semantics=("arbitrary",),
+            vmem_limit_bytes=60 * 1024 * 1024,
+        )
+
+    smem = pl.BlockSpec(memory_space=pltpu.SMEM)
+    consts = (
+        gain_one, shift_one, w_qkv, bias_qv, w_proj, b_proj,
+        gain_two, shift_two, w_up, b_up, w_down, b_down,
+    )
+    lefts_width = 3 * width + hidden
+    rights_width = 5 * width + hidden
+    outputs, held, lefts, qkv, slope, mid = pl.pallas_call(
+        forward_kernel,
+        grid=(micro,),
+        out_shape=(
+            jax.ShapeDtypeStruct((micro, tokens, width), low),
+            jax.ShapeDtypeStruct((micro, rows, width), low),
+            jax.ShapeDtypeStruct((micro, rows, lefts_width), low),
+            jax.ShapeDtypeStruct((micro, rows, 3 * width), low),
+            jax.ShapeDtypeStruct((micro, rows, hidden), jnp.float32),
+            jax.ShapeDtypeStruct((micro, rows, width), jnp.float32),
+        ),
+        in_specs=[smem, per_step(ahead, 1, tokens, width)] + [fixed(x) for x in consts],
+        out_specs=(
+            per_step(ahead, tokens, width),
+            per_step(ahead, rows, width),
+            per_step(ahead, rows, lefts_width),
+            per_step(ahead, rows, 3 * width),
+            per_step(ahead, rows, hidden),
+            per_step(ahead, rows, width),
+        ),
+        scratch_shapes=[
+            pltpu.VMEM((micro, rows, width), low),
+            pltpu.VMEM((micro, rows, width), low),
+            dma((micro,)),
+            dma((micro,)),
+        ],
+        compiler_params=params(1),
+    )(keeps, inputs, *consts)
+    small_rows = 8 + hidden // width
+    small_rows += -small_rows % 8
+    consts = (gain_one, w_qkv, w_proj, gain_two, w_up, w_down)
+    d_inputs, rights, small = pl.pallas_call(
+        backward_kernel,
+        grid=(micro,),
+        out_shape=(
+            jax.ShapeDtypeStruct((micro, tokens, width), low),
+            jax.ShapeDtypeStruct((micro, rows, rights_width), low),
+            jax.ShapeDtypeStruct((small_rows, width), jnp.float32),
+        ),
+        in_specs=[
+            smem,
+            per_step(back, 1, tokens, width),
+            per_step(back, rows, width),
+            per_step(back, rows, 3 * width),
+            per_step(back, rows, hidden),
+            per_step(back, rows, width),
+        ]
+        + [fixed(x) for x in consts],
+        out_specs=(
+            per_step(back, tokens, width),
+            per_step(back, rows, rights_width),
+            pl.BlockSpec((small_rows, width), lambda i: (0, 0)),
+        ),
+        scratch_shapes=[
+            pltpu.VMEM((micro, rows, width), low),
+            pltpu.VMEM((micro, rows, width), low),
+            pltpu.VMEM((1, rows, width), low),
+            pltpu.VMEM((rows, width), low),
+            dma((micro,)),
+            dma((micro,)),
+        ],
+        compiler_params=params(2),
+    )(keeps, cotangent, held, qkv, slope, mid, *consts)
+    return (
+        outputs,
+        d_inputs,
+        lefts.reshape(micro * rows, lefts_width),
+        rights.reshape(micro * rows, rights_width),
+        small,
+    )
 
 
 COLS = 256
@@ -453,7 +671,8 @@
 
             @pl.when(u0 == chunks)
             def _():
-                partial[s0] = small_ref[...]
+                partial[s0] = jnp.zeros(partial.shape[1:], jnp.float32)
+                partial[s0, 0] = small_ref[...]
 
             give[s0] = partial[s0, pl.ds((1 - core) * half, half)].astype(jnp.bfloat16)
             to_core(s0).start()
@@ -465,13 +684,14 @@
 
 def sum_weight_grads(lefts, rights, small, width):
     count = lax.axis_size("dp")
+    small = small.reshape(-1)
     hidden = rights.shape[1] - 5 * width
     piece = width // count
-    if width % COLS or count % 4 or width % (16 * count) or small.size > width * COLS:
+    if width % COLS or count % 4 or width % (16 * count) or small.size > piece * COLS:
         return sum_weight_grads_plain(lefts, rights, small, width)
     line = count // 4
     tile = (count, piece, COLS)
-    small_in = jnp.pad(small, (0, width * COLS - small.size)).reshape(tile)
+    small_in = jnp.pad(small, (0, piece * COLS - small.size)).reshape(piece, COLS)
     low, dma = (jnp.bfloat16, pltpu.SemaphoreType.DMA)
     anywhere = pl.BlockSpec(memory_space=pl.ANY)
     vmem = pl.BlockSpec(memory_space=pltpu.VMEM)
@@ -519,7 +739,7 @@
         proj.reshape(width, width),
         up.reshape(width, hidden),
         down.reshape(hidden, width),
-        small_sum.reshape(-1)[: small.size],
+        small_sum[0].reshape(-1)[: small.size],
     )
 
 
@@ -583,51 +803,12 @@
             )
         )
     )
-    section_index = lax.axis_index("section")
-    first = section_index == 0
-    micro = inputs.shape[0]
-    keep_scaled = keep_masks[0].astype(jnp.float32) * survive
-
-    def keeps_for(index):
-        clipped = jnp.clip(index, 0, micro - 1)
-        return lax.dynamic_index_in_dim(keep_scaled, clipped, 1, keepdims=False)
-
-    received = jnp.zeros_like(inputs[0])
-    kept_inputs = []
-    results = []
-    for tick in range(micro + 1):
-        own = inputs[min(tick, micro - 1)]
-        layer_in = jnp.where(first, own, received)
-        kept_inputs.append(layer_in)
-        result = run_forward(layer_in, weights, keeps_for(tick - section_index))[0]
-        results.append(result)
-        if tick < micro:
-            received = from_behind(result, "section", 1)
-    layer_outputs = jnp.where(first, jnp.stack(results[:micro]), jnp.stack(results[1:]))[None]
-    returned = jnp.zeros_like(inputs[0])
-    grads_in = []
-    lefts, rights = ([], [])
-    small_total = None
-    for tick in range(micro + 1):
-        index = micro - tick - section_index
-        valid = (index >= 0) & (index < micro)
-        own = cotangent[max(micro - 1 - tick, 0)]
-        upstream = jnp.where(first, returned, own)
-        upstream = jnp.where(valid, upstream, jnp.zeros_like(upstream))
-        d_in, left, right, small = run_backward(
-            kept_inputs[micro - tick], weights, keeps_for(index), upstream
-        )
-        grads_in.append(d_in)
-        if tick < micro:
-            returned = from_behind(d_in, "section", -1)
-        pad = -left.shape[0] % 16
-        lefts.append(jnp.pad(left, ((0, pad), (0, 0))))
-        rights.append(jnp.pad(right, ((0, pad), (0, 0))))
-        small_total = small if small_total is None else small_total + small
-    lefts = jnp.concatenate(lefts)
-    rights = jnp.concatenate(rights)
+    keeps = keep_masks[0, :, :, 0].astype(jnp.float32) * survive
+    outputs, d_inputs, lefts, rights, small = run_layers(inputs, cotangent, weights, keeps)
+    layer_outputs = outputs[None, :, None]
+    input_grads = d_inputs[None, :, None]
     width = inputs.shape[-1]
-    qkv, proj, up, down, small = sum_weight_grads(lefts, rights, small_total, width)
+    qkv, proj, up, down, small = sum_weight_grads(lefts, rights, small, width)
     hidden = up.shape[1]
     sizes = (width, width, 2 * width, width, width, width, hidden, width)
     starts = [sum(sizes[:i]) for i in range(len(sizes))]
@@ -636,9 +817,6 @@
         parts[0], parts[1], qkv, parts[2], proj, parts[3],
         parts[4], parts[5], up, parts[6], down, parts[7],
     )
-    input_grads = jnp.where(
-        first, jnp.stack(grads_in[1:][::-1]), jnp.stack(grads_in[:micro][::-1])
-    )[None]
     return (
         layer_outputs,
         input_grads,

time: 767 us -> 381 us (0.50); the launches traced: 754 us -> 380 us
  matrix products: 203 us -> 0 us
  local copies, waits for them, and re-layouts: 178 us -> 17 us
  Pallas kernels: 233 us -> 344 us
  other arithmetic: 97.4 us -> 18.9 us
  starting transfers between devices: 24 us -> 0 us
  waiting for transfers between devices: 14.2 us -> 0 us
    dot_general x65 -> x0, matrix products: 182 us -> none  [the longest x5 44.8 us: run_forward(): u_val = jnp.dot(c_low, w_up, preferred_element_type=jnp.float32) + b_up]
    pallas_call x0 -> x2, Pallas kernels: none -> 115 us  [the longest x1 71.5 us: run_layers(): pl.pallas_call(backward_kernel, grid=(micro,), out_shape=(jax.ShapeDtypeS...]
    unnamed x606 -> x23, local copies, waits for them, and re-layouts: 75.9 us -> 15.6 us
    reshape x21 -> x1, local copies, waits for them, and re-layouts: 39.8 us -> 1.43 us  [sum_weight_grads(): jnp.pad(small, (0, piece * COLS - small.size)).reshape(piece, COLS)]
    reduce_sum x30 -> x0, other arithmetic: 35.1 us -> none  [the longest x5 12.1 us: run_backward(): grad_proj_bias = jnp.sum(d_branch.astype(jnp.float32), axis=0)]
    convert_element_type x15 -> x0, local copies, waits for them, and re-layouts: 28.4 us -> none  [the longest x5 9.49 us: run_forward(): value = (qkv[:, 2 * width:] + bias_qv[width:]).astype(jnp.bfloat16).resha...]
    ppermute x8 -> x0, starting transfers between devices: 24 us -> none  [from_behind(): lax.ppermute(value, axis, [(source, source + steps) for source in range(i...]
    slice x17 -> x0, local copies, waits for them, and re-layouts: 23.7 us -> none  [the longest x10 13.2 us: run_forward(): qkv[:, width:2 * width].astype(jnp.bfloat16)]
  transfers between devices with their start and end apart: 8 -> 0, of which waited for: 3 -> 0; matrix products, arithmetic and copies ran while one was open for 7% -> 0% of each run, Pallas kernels for 0% -> 0%
where the time goes in v2:
time: 381 us; the launch traced here: 380 us
  Pallas kernels  344 us (90%)
  other arithmetic  18.9 us (5%)
  local copies, waits for them, and re-layouts  17 us (4%)
    pallas_call x1, Pallas kernels, sum_weight_grads(): pl.pallas_call(functools.partial(reduce_kernel, count, width, hidden), ou...  229 us
    pallas_call x1, Pallas kernels, run_layers(): pl.pallas_call(backward_kernel, grid=(micro,), out_shape=(jax.ShapeDtypeS...  71.5 us
    pallas_call x1, Pallas kernels, run_layers(): pl.pallas_call(forward_kernel, grid=(micro,), out_shape=(jax.ShapeDtypeSt...  43.4 us
    unnamed x23, local copies, waits for them, and re-layouts  15.6 us

profile of v2, /device:TPU:1, one launch (start us, length us, event | category | flops | bytes accessed | tf_op | source)
XLA Modules:
  0.0 380.3 jit_solution(7991692877251559285)
XLA Ops:
  0.6 1.2 convert_multiply_fusion
  1.9 2.4 copy.33.in_ref
  4.3 2.4 copy.34.cot_ref
  6.8 43.4 %shard_map.254 = (bf16[4,198,768]{2,1,0:T(8,128)(2,1)}, bf16[4,208,768]{2,1,0:T(8,128)(2,1)}, bf16[4,208,5376]{2,1,0:T(8,128)(2,1)}, bf16[4,208,2304]{2,1,0:T(8,...) custom-call(f32[2,4]{1,0:T(2,128)} %bitcast.66, bf16[4,1,198,768]{3,2,1,0:T(8,128)(2,1)} %copy.33.in_ref, ...), custom_call_target="tpu_custom_call" | custom-call | tf_op jit(solution)/shard_map/pallas_call | solution.py:360
  50.2 2.8 copy.35
  52.9 71.5 %shard_map.255 = (bf16[4,198,768]{2,1,0:T(8,128)(2,1)}, bf16[4,208,6912]{2,1,0:T(8,128)(2,1)}, f32[16,768]{1,0:T(8,128)}) custom-call(f32[2,4]{1,0:T(2,128)} %bitcast.67, bf16[4,1,198,768]{3,2,1,0:T(8,128)(2,1)} %copy.34.cot_ref, bf16[4,208,768]{2,1,0:T(8,128)(2,1)} %get-tuple-element.29.held_ref, bf16[4,208,2304]{2,1,0:T(8,128)(2,1)} %get-tuple-element.30.qkv_ref, ...), custom_call_target="tpu_custom_call" | custom-call | tf_op jit(solution)/shard_map/pallas_call | solution.py:391
  124.5 2.8 copy.36
  127.3 1.4 reshape.60.small_ref
  128.7 228.7 %shard_map.256 = (bf16[16,48,2304]{2,1,0:T(8,128)(2,1)}, bf16[16,48,768]{2,1,0:T(8,128)(2,1)}, bf16[16,48,3072]{2,1,0:T(8,128)(2,1)}, bf16[4,16,48,768]{3,2,1,0:T(8,128)(2,1)}, bf16[16,48,256]{2,1,0:T(8,128)(2,1)}) custom-call(bf16[832,5376]{1,0:T(8,128)(2,1)} %bitcast.54, bf16[832,6912]{1,0:T(8,128)(2,1)} %bitcast.53, f32[48,256]{1,0:T(8,128)} %reshape.60.small_ref), custom_call_target="tpu_custom_call" | custom-call | tf_op jit(solution)/shard_map/pallas_call | solution.py:698
  357.4 0.0 copy-start.1
  357.4 1.2 convert_element_type.12
  358.6 0.6 copy.39
  359.2 0.6 copy.43
  359.9 0.6 copy.44
  360.4 0.6 copy.42
  361.0 0.6 copy.41
  361.6 0.6 copy.40
  362.2 0.6 copy.38
  362.8 0.6 copy.37
  363.3 2.8 bitcast_convert_fusion.2
  366.2 0.0 copy-done.1
  366.2 0.0 copy-start
  366.2 0.0 slice-start
  366.2 4.1 %bitcast_convert_fusion.1 = f32[1,768,2304]{2,1,0:T(8,128)} fusion(bf16[1,768,2304]{2,1,0:T(8,128)(2,1)S(1)} %bitcast.61), kind=kLoop, calls=%fused_computation.1 | loop fusion | flops 1769472 | bytes 10616832 | tf_op jit(solution)/shard_map/broadcast_in_dim;reshape | solution.py:825
  370.3 0.4 copy-done
  370.7 0.0 slice-start.1
  370.7 5.0 %bitcast_convert_fusion = f32[1,768,3072]{2,1,0:T(8,128)} fusion(bf16[1,768,3072]{2,1,0:T(8,128)(2,1)S(1)} %bitcast.58), kind=kLoop, calls=%fused_computation | loop fusion | flops 2359296 | bytes 14155776 | tf_op jit(solution)/shard_map/broadcast_in_dim;reshape | solution.py:831
  375.8 0.0 slice-done
  375.8 0.0 slice-done.1
  375.8 4.5 %convert.7 = f32[1,3072,768]{2,1,0:T(8,128)} convert(bf16[1,3072,768]{2,1,0:T(8,128)(2,1)S(1)} %bitcast.57) | non-fusion elementwise | flops 2359296 | bytes 14155776 | tf_op jit(solution)/shard_map/broadcast_in_dim;reshape | solution.py:833
  (4 shorter events, 0.0 us)
Async XLA Ops:
  357.4 8.8 %copy-start.1 = (bf16[16,48,2304]{2,1,0:T(8,128)(2,1)S(1)}, bf16[16,48,2304]{2,1,0:T(8,128)(2,1)}, u32[]{:S(2)}) copy-start(bf16[16,48,2304]{2,1,0:T(8,128)(2,1)} %get-tuple-element.38) | copy-start | bytes 10616836
  366.2 4.5 %copy-start = (bf16[16,48,3072]{2,1,0:T(8,128)(2,1)S(1)}, bf16[16,48,3072]{2,1,0:T(8,128)(2,1)}, u32[]{:S(2)}) copy-start(bf16[16,48,3072]{2,1,0:T(8,128)(2,1)} %get-tuple-element.40) | copy-start | bytes 14155780
  366.2 9.6 %slice-start = ((s8[4718592]{0:T(1024)(128)(4,1)}), s8[4194304]{0:T(1024)(128)(4,1)S(1)}, s32[]{:S(2)}) async-start(s8[4718592]{0:T(1024)(128)(4,1)} %bitcast.55), calls=%async_computation | async-start | bytes 8388608
  370.7 5.1 %slice-start.1 = ((s8[4718592]{0:T(1024)(128)(4,1)}), s8[524288]{0:T(1024)(128)(4,1)S(1)}, s32[]{:S(2)}) async-start(s8[4718592]{0:T(1024)(128)(4,1)} %bitcast.55), calls=%async_computation.1 | async-start | bytes 1048576

commit v3 on v2

--- a/solution.py
+++ b/solution.py
@@ -29,10 +29,33 @@
     pl.semaphore_wait(barrier, 1)
 
 
+def kept(keeps_ref, branch, m):
+    return keeps_ref[branch, m].astype(jnp.float32) * survive
+
+
 def norm_stats(values):
     centered = values - jnp.mean(values, axis=-1, keepdims=True)
     factor = lax.rsqrt(jnp.mean(centered * centered, axis=-1, keepdims=True) + epsilon)
     return (centered * factor, factor)
+
+
+def loader(first, sems, pairs):
+    copies = {
+        name: pltpu.make_async_copy(src, dst, sems.at[i])
+        for i, (name, (src, dst)) in enumerate(pairs.items())
+    }
+
+    @pl.when(first)
+    def _():
+        for copy in copies.values():
+            copy.start()
+
+    def need(name):
+        @pl.when(first)
+        def _():
+            copies[name].wait()
+
+    return need
 
 
 def dot_nn(a, b):
@@ -92,9 +115,19 @@
     send,
     send_sem,
     recv_sem,
+    v_qkv,
+    v_proj,
+    v_up,
+    v_down,
+    load_sem,
 ):
     m = pl.program_id(0)
     micro = pl.num_programs(0)
+    need = loader(
+        m == 0,
+        load_sem,
+        {"qkv": (w_qkv, v_qkv), "proj": (w_proj, v_proj), "up": (w_up, v_up), "down": (w_down, v_down)},
+    )
     section = lax.axis_index("section")
     peer = {"section": 1 - section}
     tokens, width = y_ref.shape[1:]
@@ -128,9 +161,10 @@
     normed, _ = norm_stats(h)
     a_low = (normed * ln1_gain[...] + ln1_bias[...]).astype(jnp.bfloat16)
     left_ref[0, :, 0:width] = a_low
+    need("qkv")
     for part in range(3):
         span = slice(part * width, (part + 1) * width)
-        product = dot_nn(a_low, w_qkv[:, span])
+        product = dot_nn(a_low, v_qkv[:, span])
         if part == 0:
             product = product + qv_bias[:, 0:width]
         if part == 2:
@@ -150,23 +184,26 @@
             joined = one if joined is None else joined + one
         left_ref[0, :, width + p * pair : width + (p + 1) * pair] = joined.astype(jnp.bfloat16)
 
-    branch = dot_nn(left_ref[0, :, width : 2 * width], w_proj[...]) + b_proj[...]
-    x_mid = h + keeps_ref[0, m] * branch
+    need("proj")
+    branch = dot_nn(left_ref[0, :, width : 2 * width], v_proj[...]) + b_proj[...]
+    x_mid = h + kept(keeps_ref, 0, m) * branch
     mid_ref[0] = x_mid
     normed, _ = norm_stats(x_mid)
     c_low = (normed * ln2_gain[...] + ln2_bias[...]).astype(jnp.bfloat16)
     left_ref[0, :, 2 * width : 3 * width] = c_low
+    need("up")
+    need("down")
     total = None
     for part in range(hidden // width):
         span = slice(part * width, (part + 1) * width)
-        u = dot_nn(c_low, w_up[:, span]) + b_up[:, span]
+        u = dot_nn(c_low, v_up[:, span]) + b_up[:, span]
         normal = 0.5 * (1.0 + lax.erf(u * math.sqrt(0.5)))
         slope_ref[0, :, span] = normal + u * jnp.exp(-0.5 * u * u) * (1.0 / math.sqrt(2.0 * math.pi))
         g_low = (u * normal).astype(jnp.bfloat16)
         left_ref[0, :, (3 + part) * width : (4 + part) * width] = g_low
-        one = dot_nn(g_low, w_down[span, :])
+        one = dot_nn(g_low, v_down[span, :])
         total = one if total is None else total + one
-    y = (x_mid + keeps_ref[1, m] * (total + b_down[...])).astype(jnp.bfloat16)
+    y = (x_mid + kept(keeps_ref, 1, m) * (total + b_down[...])).astype(jnp.bfloat16)
     y_ref[0] = y[0:tokens]
 
     @pl.when(section == 0)
@@ -202,6 +239,7 @@
     d_heads,
     send_sem,
     recv_sem,
+    total_small,
 ):
     j = pl.program_id(0)
     micro = pl.num_programs(0)
@@ -217,7 +255,7 @@
     @pl.when(j == 0)
     def _():
         meet(peer)
-        small_ref[...] = jnp.zeros_like(small_ref)
+        total_small[...] = jnp.zeros_like(total_small)
 
     def copy_of(i):
         return pltpu.make_async_remote_copy(
@@ -239,9 +277,9 @@
         upstream[0] = recv[j]
 
     def add_small(row, values):
-        small_ref[row : row + 1, :] += jnp.sum(values, axis=0, keepdims=True)
-
-    keep_attn, keep_mlp = (keeps_ref[0, m], keeps_ref[1, m])
+        total_small[row : row + 1, :] += jnp.sum(values, axis=0, keepdims=True)
+
+    keep_attn, keep_mlp = (kept(keeps_ref, 0, m), kept(keeps_ref, 1, m))
     d_end = upstream[0].astype(jnp.float32)
     dm_low = (d_end * keep_mlp).astype(jnp.bfloat16)
     first_up = 4 * width
@@ -314,6 +352,15 @@
         send[j] = d_low
         copy_of(j).start()
 
+    @pl.when(j == micro - 1)
+    def _():
+        lines = width // COLS
+        for row in range(total_small.shape[0]):
+            for i in range(lines):
+                small_ref[row * lines + i : row * lines + i + 1, :] = total_small[
+                    row : row + 1, i * COLS : (i + 1) * COLS
+                ]
+
     @pl.when((section == 1) & (j == micro - 1))
     def _():
         for i in range(send.shape[0]):
@@ -351,6 +398,12 @@
         )
 
     smem = pl.BlockSpec(memory_space=pltpu.SMEM)
+    big = (w_qkv, w_proj, w_up, w_down)
+    loads = [pltpu.VMEM(w.shape, low) for w in big] + [dma((len(big),))]
+
+    def weight(x):
+        return pl.BlockSpec(memory_space=pl.ANY) if any(x is w for w in big) else fixed(x)
+
     consts = (
         gain_one, shift_one, w_qkv, bias_qv, w_proj, b_proj,
         gain_two, shift_two, w_up, b_up, w_down, b_down,
@@ -368,7 +421,7 @@
             jax.ShapeDtypeStruct((micro, rows, hidden), jnp.float32),
             jax.ShapeDtypeStruct((micro, rows, width), jnp.float32),
         ),
-        in_specs=[smem, per_step(ahead, 1, tokens, width)] + [fixed(x) for x in consts],
+        in_specs=[smem, per_step(ahead, 1, tokens, width)] + [weight(x) for x in consts],
         out_specs=(
             per_step(ahead, tokens, width),
             per_step(ahead, rows, width),
@@ -382,7 +435,8 @@
             pltpu.VMEM((micro, rows, width), low),
             dma((micro,)),
             dma((micro,)),
-        ],
+        ]
+        + loads,
         compiler_params=params(1),
     )(keeps, inputs, *consts)
     small_rows = 8 + hidden // width
@@ -394,7 +448,7 @@
         out_shape=(
             jax.ShapeDtypeStruct((micro, tokens, width), low),
             jax.ShapeDtypeStruct((micro, rows, rights_width), low),
-            jax.ShapeDtypeStruct((small_rows, width), jnp.float32),
+            jax.ShapeDtypeStruct((small_rows * width // COLS, COLS), jnp.float32),
         ),
         in_specs=[
             smem,
@@ -408,7 +462,7 @@
         out_specs=(
             per_step(back, tokens, width),
             per_step(back, rows, rights_width),
-            pl.BlockSpec((small_rows, width), lambda i: (0, 0)),
+            pl.BlockSpec((small_rows * width // COLS, COLS), lambda i: (0, 0)),
         ),
         scratch_shapes=[
             pltpu.VMEM((micro, rows, width), low),
@@ -417,6 +471,7 @@
             pltpu.VMEM((rows, width), low),
             dma((micro,)),
             dma((micro,)),
+            pltpu.VMEM((small_rows, width), jnp.float32),
         ],
         compiler_params=params(2),
     )(keeps, cotangent, held, qkv, slope, mid, *consts)
@@ -430,16 +485,20 @@
 
 
 COLS = 256
-SLOTS = 8
-LAST = 7
+SLOTS = 16
+PARTIALS = 8
+
+
+DELAYS = (0, 1, 3, 5, 7, 9, 11, 13, 14, 15)
+HOPS = 14
 
 
 def reduce_kernel(
     count,
     width,
     hidden,
-    left_ref,
-    right_ref,
+    left_hbm,
+    right_hbm,
     small_ref,
     qkv_ref,
     proj_ref,
@@ -447,100 +506,118 @@
     down_ref,
     small_out,
     partial,
-    give,
-    give_x,
-    give_z,
-    take,
-    take_x,
-    take_z,
+    give_core,
+    take_core,
+    give_ax,
+    take_ax,
+    give_be,
+    take_be,
+    give_ae,
+    take_ae,
+    give_bm,
+    take_bm,
+    give_am,
+    take_am,
+    give_bx,
+    take_bx,
     whole,
-    sent_core,
-    sent_x,
-    sent_z,
-    spread_z,
-    spread_x,
-    spread_core,
-    got_core,
-    got_x,
-    got_z,
-    held_z,
-    held_x,
-    held_core,
+    send_sem,
+    recv_sem,
     out_sem,
+    left_ref,
+    right_ref,
+    left_sem,
+    right_sem,
 ):
-    line = count // 4
     per = width // COLS
-    up_chunks = hidden // COLS
     first_proj, first_up = (3 * per, 4 * per)
-    first_down = first_up + up_chunks
+    first_down = first_up + hidden // COLS
     chunks = first_down + per * (hidden // width)
     me = lax.axis_index("dp")
     core = lax.rem(me, 2)
-    chip = me // 2
-    across = lax.rem(chip, 2)
-    along = chip // 2
-    half = 2 * line
+    across = lax.rem(me // 2, 2)
+    along = me // 4
+    side = along // 2
+    at_end = (along == 0) | (along == 3)
+    at_middle = (along == 1) | (along == 2)
 
     def device(z, x, k):
         return {"dp": (z * 2 + x) * 2 + k}
 
     other_core = device(along, across, 1 - core)
     other_x = device(along, 1 - across, core)
-    others_z = [device(lax.rem(along + i, line), across, core) for i in range(1, line)]
+    other_pair = device(along + 1 - 2 * lax.rem(along, 2), across, core)
+    other_middle = device(3 - along, across, core)
+
+    def load(src, dst, sem, block):
+        columns = pl.ds(pl.multiple_of(block * width, width), width)
+        return pltpu.make_async_copy(src.at[:, columns], dst.at[:, columns], sem.at[block])
+
+    def load_left(block):
+        return load(left_hbm, left_ref, left_sem, block)
+
+    def load_right(block):
+        return load(right_hbm, right_ref, right_sem, block)
+
+    downs = hidden // width
+    lefts_of = [0] * 3 + [1] + [2] * downs + list(range(3, 3 + downs))
+    rights_of = list(range(4 + downs)) + [4 + downs] * downs
+    for i, (left, right) in enumerate(zip(lefts_of, rights_of)):
+        if left not in lefts_of[:i]:
+            load_left(left).start()
+        if right not in rights_of[:i]:
+            load_right(right).start()
 
     barrier = pltpu.get_barrier_semaphore()
-    for peer in [other_core, other_x] + others_z:
+    for peer in (other_core, other_x, other_pair, other_middle):
         pl.semaphore_signal(barrier, inc=1, device_id=peer, device_id_type=pl.DeviceIdType.MESH)
-    pl.semaphore_wait(barrier, 1 + line)
-
-    own_half = core * half
-    own_quarter = own_half + across * line
-    own_piece = own_quarter + along
-
-    def remote(src, dst, send, recv, peer):
-        return pltpu.make_async_remote_copy(
-            src_ref=src,
-            dst_ref=dst,
-            send_sem=send,
-            recv_sem=recv,
-            device_id=peer,
-            device_id_type=pl.DeviceIdType.MESH,
-        )
-
-    def to_core(s):
-        return remote(give.at[s], take.at[s], sent_core.at[s], got_core.at[s], other_core)
-
-    def to_x(s):
-        return remote(give_x.at[s], take_x.at[s], sent_x.at[s], got_x.at[s], other_x)
-
-    def to_z(s):
-        return [
-            remote(
-                give_z.at[s, lax.rem(along + i, line)],
-                take_z.at[s, i - 1],
-                sent_z.at[s, i - 1],
-                got_z.at[s, i - 1],
-                others_z[i - 1],
+    pl.semaphore_wait(barrier, 4)
+
+    lanes_a, lanes_b = (pl.ds(0, COLS // 2), pl.ds(COLS // 2, COLS // 2))
+    half = core * 8
+    a_part, a_other = (half + across * 4, half + (1 - across) * 4)
+    a_mine, a_theirs = (a_part + side * 2, a_part + (1 - side) * 2)
+    b_part, b_other = (half + side * 4, half + (1 - side) * 4)
+    b_mine, b_theirs = (b_part + across * 2, b_part + (1 - across) * 2)
+
+    def hop(number, src, dst, peer):
+        def at(s):
+            return pltpu.make_async_remote_copy(
+                src_ref=src(s),
+                dst_ref=dst(s),
+                send_sem=send_sem.at[number, s],
+                recv_sem=recv_sem.at[number, s],
+                device_id=peer,
+                device_id_type=pl.DeviceIdType.MESH,
             )
-            for i in range(1, line)
-        ]
-
-    def back_z(s):
-        piece = whole.at[s, own_piece]
-        return [
-            remote(
-                piece, piece, spread_z.at[s, i - 1], held_z.at[s, i - 1], others_z[i - 1]
-            )
-            for i in range(1, line)
-        ]
-
-    def back_x(s):
-        part = whole.at[s, pl.ds(own_quarter, line)]
-        return remote(part, part, spread_x.at[s], held_x.at[s], other_x)
-
-    def back_core(s):
-        part = whole.at[s, pl.ds(own_half, half)]
-        return remote(part, part, spread_core.at[s], held_core.at[s], other_core)
+
+        return at
+
+    def slot_of(ref):
+        return lambda s: ref.at[s]
+
+    def pieces(start, size, lanes=None):
+        if lanes is None:
+            return lambda s: whole.at[s, pl.ds(start, size)]
+        return lambda s: whole.at[s, pl.ds(start, size), :, lanes]
+
+    def spread(number, part, peer):
+        return hop(number, part, part, peer)
+
+    core_hop = hop(0, slot_of(give_core), slot_of(take_core), other_core)
+    ax_hop = hop(1, slot_of(give_ax), slot_of(take_ax), other_x)
+    be_hop = hop(2, slot_of(give_be), slot_of(take_be), other_pair)
+    ae_hop = hop(3, slot_of(give_ae), slot_of(take_ae), other_pair)
+    bm_hop = hop(4, slot_of(give_bm), slot_of(take_bm), other_middle)
+    am_hop = hop(5, slot_of(give_am), slot_of(take_am), other_middle)
+    bx_hop = hop(6, slot_of(give_bx), slot_of(take_bx), other_x)
+    am_back = spread(7, pieces(a_mine, 2, lanes_a), other_middle)
+    bx_back = spread(8, pieces(b_mine, 2, lanes_b), other_x)
+    ae_back = spread(9, pieces(a_part, 4, lanes_a), other_pair)
+    bm_back = spread(10, pieces(b_part, 4, lanes_b), other_middle)
+    ax_back = spread(11, pieces(a_part, 4, lanes_a), other_x)
+    be_back = spread(12, pieces(half, 8, lanes_b), other_pair)
+    core_back = spread(13, pieces(half, 8), other_core)
 
     def for_output(u, s, act):
         def go(ref, row, column):
@@ -568,118 +645,170 @@
         def _():
             go(small_out, None, 0)
 
+    def low(x):
+        return x.astype(jnp.bfloat16)
+
+    def wide(x):
+        return x.astype(jnp.float32)
+
+    def products(u, p):
+        def reached(k):
+            return (u + chunks - k) // chunks
+
+        block = reached(first_proj) + reached(first_up)
+        column = u
+        for row in range(downs):
+            past = reached(first_down + per * row)
+            block = block + past
+            column = column - per * past if row else column
+        fresh = lax.rem(u, per) == 0
+
+        @pl.when((u == 0) | (u == first_proj) | (u == first_up) | (fresh & (u >= first_down)))
+        def _():
+            load_left(block).wait()
+
+        @pl.when(fresh & (u <= first_down))
+        def _():
+            load_right(u // per).wait()
+
+        rows = pl.ds(pl.multiple_of(block * width, width), width)
+        columns = pl.ds(pl.multiple_of(column * COLS, COLS), COLS)
+        product = dot_tn(left_ref[:, rows], right_ref[:, columns])
+        partial[p] = product.reshape(partial.shape[1:])
+
+    def add(p, start, size, lanes, found):
+        part = (p, pl.ds(start, size), slice(None), lanes)
+        total = partial[part] + wide(found)
+        partial[part] = total
+        return total
+
     def step(t, carry):
-        def stage(delay):
-            u = t - delay
-            return u, lax.rem(u + SLOTS, SLOTS), (u >= 0) & (u <= chunks)
-
-        u7, s7, on7 = stage(7)
-
-        @pl.when(on7)
-        def _():
-            for_output(u7, s7, lambda copy: copy.wait())
-            to_core(s7).wait_send()
-            to_x(s7).wait_send()
-            for copy in to_z(s7) + back_z(s7):
-                copy.wait_send()
-            back_x(s7).wait_send()
-            back_core(s7).wait_send()
-
-        u6, s6, on6 = stage(6)
-
-        @pl.when(on6)
-        def _():
-            back_core(s6).wait_recv()
-            for_output(u6, s6, lambda copy: copy.start())
-
-        u5, s5, on5 = stage(5)
-
-        @pl.when(on5)
-        def _():
-            back_x(s5).wait_recv()
-            back_core(s5).start()
-
-        u4, s4, on4 = stage(4)
-
-        @pl.when(on4)
-        def _():
-            for copy in back_z(s4):
-                copy.wait_recv()
-            back_x(s4).start()
-
-        u3, s3, on3 = stage(3)
-
-        @pl.when(on3)
-        def _():
-            for copy in to_z(s3):
-                copy.wait_recv()
-            total = partial[s3, own_piece]
-            for i in range(line - 1):
-                total = total + take_z[s3, i].astype(jnp.float32)
-            whole[s3, own_piece] = total.astype(jnp.bfloat16)
-            for copy in back_z(s3):
-                copy.start()
-
-        u2, s2, on2 = stage(2)
-
-        @pl.when(on2)
-        def _():
-            to_x(s2).wait_recv()
-            quarter = pl.ds(own_quarter, line)
-            total = partial[s2, quarter] + take_x[s2].astype(jnp.float32)
-            partial[s2, quarter] = total
-            give_z[s2] = total.astype(jnp.bfloat16)
-            for copy in to_z(s2):
-                copy.start()
-
-        u1, s1, on1 = stage(1)
-
-        @pl.when(on1)
-        def _():
-            to_core(s1).wait_recv()
-            mine = pl.ds(own_half, half)
-            partial[s1, mine] = partial[s1, mine] + take[s1].astype(jnp.float32)
-            give_x[s1] = partial[s1, pl.ds(own_half + (1 - across) * line, line)].astype(
-                jnp.bfloat16
-            )
-            to_x(s1).start()
-
-        u0, s0, on0 = stage(0)
-
-        @pl.when(on0)
-        def _():
-            @pl.when(u0 < chunks)
+        def stage(number, when=None):
+            u = t - DELAYS[number]
+            active = (u >= 0) & (u <= chunks)
+            if when is not None:
+                active = active & when
+            s, p = (lax.rem(u + SLOTS, SLOTS), lax.rem(u + SLOTS, PARTIALS))
+            return lambda body: pl.when(active)(lambda: body(u, s, p))
+
+        @stage(9)
+        def _(u, s, p):
+            for_output(u, s, lambda copy: copy.wait())
+            for copy in (core_hop, ax_hop, ax_back, core_back):
+                copy(s).wait_send()
+
+        @stage(9, at_end)
+        def _(u, s, p):
+            be_hop(s).wait_send()
+            ae_hop(s).wait_send()
+
+        @stage(9, at_middle)
+        def _(u, s, p):
+            for copy in (bm_hop, am_hop, bx_hop, am_back, bx_back, ae_back, bm_back, be_back):
+                copy(s).wait_send()
+
+        @stage(8)
+        def _(u, s, p):
+            core_back(s).wait_recv()
+            for_output(u, s, lambda copy: copy.start())
+
+        @stage(7, at_end)
+        def _(u, s, p):
+            be_back(s).wait_recv()
+
+        @stage(7)
+        def _(u, s, p):
+            ax_back(s).wait_recv()
+            core_back(s).start()
+
+        @stage(6, at_end)
+        def _(u, s, p):
+            ae_back(s).wait_recv()
+
+        @stage(6, at_middle)
+        def _(u, s, p):
+            bm_back(s).wait_recv()
+            be_back(s).start()
+
+        @stage(6)
+        def _(u, s, p):
+            ax_back(s).start()
+
+        @stage(5, at_middle)
+        def _(u, s, p):
+            am_back(s).wait_recv()
+            ae_back(s).start()
+            bx_back(s).wait_recv()
+            bm_back(s).start()
+
+        @stage(4, at_middle)
+        def _(u, s, p):
+            am_hop(s).wait_recv()
+            mine = pl.ds(a_mine, 2)
+            whole[s, mine, :, lanes_a] = low(partial[p, mine, :, lanes_a] + wide(take_am[s]))
+            am_back(s).start()
+            bx_hop(s).wait_recv()
+            mine = pl.ds(b_mine, 2)
+            whole[s, mine, :, lanes_b] = low(partial[p, mine, :, lanes_b] + wide(take_bx[s]))
+            bx_back(s).start()
+
+        @stage(3, at_middle)
+        def _(u, s, p):
+            ae_hop(s).wait_recv()
+            add(p, a_part, 4, lanes_a, take_ae[s])
+            give_am[s] = low(partial[p, pl.ds(a_theirs, 2), :, lanes_a])
+            am_hop(s).start()
+            bm_hop(s).wait_recv()
+            add(p, b_part, 4, lanes_b, take_bm[s])
+            give_bx[s] = low(partial[p, pl.ds(b_theirs, 2), :, lanes_b])
+            bx_hop(s).start()
+
+        @stage(2)
+        def _(u, s, p):
+            ax_hop(s).wait_recv()
+            total = add(p, a_part, 4, lanes_a, take_ax[s])
+
+            @pl.when(at_end)
             def _():
-                def reached(k):
-                    return (u0 + chunks - k) // chunks
-
-                block = reached(first_proj) + reached(first_up)
-                for row in range(hidden // width):
-                    block = block + reached(first_down + per * row)
-                column = u0
-                for row in range(1, hidden // width):
-                    column = column - per * reached(first_down + per * row)
-                rows = pl.ds(pl.multiple_of(block * width, width), width)
-                columns = pl.ds(pl.multiple_of(column * COLS, COLS), COLS)
-                product = lax.dot_general(
-                    left_ref[:, rows],
-                    right_ref[:, columns],
-                    (((0,), (0,)), ((), ())),
-                    preferred_element_type=jnp.float32,
-                )
-                partial[s0] = product.reshape(partial.shape[1:])
-
-            @pl.when(u0 == chunks)
+                give_ae[s] = low(total)
+                ae_hop(s).start()
+
+        @stage(2, at_middle)
+        def _(u, s, p):
+            be_hop(s).wait_recv()
+            add(p, half, 8, lanes_b, take_be[s])
+            give_bm[s] = low(partial[p, pl.ds(b_other, 4), :, lanes_b])
+            bm_hop(s).start()
+
+        @stage(1)
+        def _(u, s, p):
+            core_hop(s).wait_recv()
+            total = add(p, half, 8, slice(None), take_core[s])
+            give_ax[s] = low(partial[p, pl.ds(a_other, 4), :, lanes_a])
+            ax_hop(s).start()
+
+            @pl.when(at_end)
             def _():
-                partial[s0] = jnp.zeros(partial.shape[1:], jnp.float32)
-                partial[s0, 0] = small_ref[...]
-
-            give[s0] = partial[s0, pl.ds((1 - core) * half, half)].astype(jnp.bfloat16)
-            to_core(s0).start()
+                give_be[s] = low(total[:, :, COLS // 2 :])
+                be_hop(s).start()
+
+        @stage(0)
+        def _(u, s, p):
+            @pl.when(u < chunks)
+            def _():
+                products(u, p)
+
+            @pl.when(u == chunks)
+            def _():
+                partial[p] = jnp.zeros(partial.shape[1:], jnp.float32)
+                partial[p, 0 : small_ref.shape[0]] = small_ref[...]
+
+            give_core[s] = low(partial[p, pl.ds((1 - core) * 8, 8)])
+            core_hop(s).start()
 
         return carry
 
-    lax.fori_loop(0, chunks + 1 + LAST, step, 0)
+    lax.fori_loop(0, chunks + 1 + DELAYS[-1], step, 0)
 
 
 def sum_weight_grads(lefts, rights, small, width):
@@ -687,11 +816,10 @@
     small = small.reshape(-1)
     hidden = rights.shape[1] - 5 * width
     piece = width // count
-    if width % COLS or count % 4 or width % (16 * count) or small.size > piece * COLS:
+    if width % COLS or count != 16 or width % (16 * count) or small.size % (piece * COLS) or small.size > width * COLS:
         return sum_weight_grads_plain(lefts, rights, small, width)
-    line = count // 4
     tile = (count, piece, COLS)
-    small_in = jnp.pad(small, (0, piece * COLS - small.size)).reshape(piece, COLS)
+    small_in = small.reshape(-1, piece, COLS)
     low, dma = (jnp.bfloat16, pltpu.SemaphoreType.DMA)
     anywhere = pl.BlockSpec(memory_space=pl.ANY)
     vmem = pl.BlockSpec(memory_space=pltpu.VMEM)
@@ -704,43 +832,78 @@
             jax.ShapeDtypeStruct((hidden // width, count, piece, width), low),
             jax.ShapeDtypeStruct(tile, low),
         ),
-        in_specs=[vmem, vmem, vmem],
+        in_specs=[anywhere, anywhere, vmem],
         out_specs=(anywhere,) * 5,
-        scratch_shapes=[
-            pltpu.VMEM((SLOTS, count, piece, COLS), jnp.float32),
-            pltpu.VMEM((SLOTS, 2 * line, piece, COLS), low),
-            pltpu.VMEM((SLOTS, line, piece, COLS), low),
-            pltpu.VMEM((SLOTS, line, piece, COLS), low),
-            pltpu.VMEM((SLOTS, 2 * line, piece, COLS), low),
-            pltpu.VMEM((SLOTS, line, piece, COLS), low),
-            pltpu.VMEM((SLOTS, line - 1, piece, COLS), low),
-            pltpu.VMEM((SLOTS, count, piece, COLS), low),
+        scratch_shapes=[pltpu.VMEM((PARTIALS,) + tile, jnp.float32)]
+        + [
+            pltpu.VMEM((SLOTS, pieces, piece, lanes), low)
+            for pieces, lanes in (
+                (8, COLS),
+                (4, COLS // 2),
+                (8, COLS // 2),
+                (4, COLS // 2),
+                (4, COLS // 2),
+                (2, COLS // 2),
+                (2, COLS // 2),
+            )
+            for _ in range(2)
+        ]
+        + [
+            pltpu.VMEM((SLOTS,) + tile, low),
+            dma((HOPS, SLOTS)),
+            dma((HOPS, SLOTS)),
             dma((SLOTS,)),
-            dma((SLOTS,)),
-            dma((SLOTS, line - 1)),
-            dma((SLOTS, line - 1)),
-            dma((SLOTS,)),
-            dma((SLOTS,)),
-            dma((SLOTS,)),
-            dma((SLOTS,)),
-            dma((SLOTS, line - 1)),
-            dma((SLOTS, line - 1)),
-            dma((SLOTS,)),
-            dma((SLOTS,)),
-            dma((SLOTS,)),
+            pltpu.VMEM(lefts.shape, low),
+            pltpu.VMEM(rights.shape, low),
+            dma((lefts.shape[1] // width,)),
+            dma((rights.shape[1] // width,)),
         ],
         compiler_params=pltpu.CompilerParams(
             collective_id=0, has_side_effects=True, vmem_limit_bytes=60 * 1024 * 1024
         ),
     )(lefts, rights, small_in)
-    qkv, proj, up, down, small_sum = (out.astype(jnp.float32) for out in outs)
-    return (
-        qkv.reshape(width, 3 * width),
-        proj.reshape(width, width),
-        up.reshape(width, hidden),
-        down.reshape(hidden, width),
-        small_sum[0].reshape(-1)[: small.size],
-    )
+    shapes = ((width, 3 * width), (width, width), (width, hidden), (hidden, width))
+    sums = [out.reshape(shape) for out, shape in zip(outs[:4], shapes)] + [outs[4]]
+    sizes = small_sizes(width, hidden)
+    steps = 8
+
+    def band(shape):
+        return pl.BlockSpec((shape[0] // steps, shape[1]), lambda i: (i, 0))
+
+    result = pl.pallas_call(
+        finish_kernel,
+        grid=(steps,),
+        out_shape=[jax.ShapeDtypeStruct(shape, jnp.float32) for shape in shapes]
+        + [jax.ShapeDtypeStruct((1, size), jnp.float32) for size in sizes],
+        in_specs=[band(shape) for shape in shapes] + [pl.BlockSpec(tile, lambda i: (0, 0, 0))],
+        out_specs=[band(shape) for shape in shapes]
+        + [pl.BlockSpec((1, size), lambda i: (0, 0)) for size in sizes],
+        compiler_params=pltpu.CompilerParams(
+            dimension_semantics=("arbitrary",), vmem_limit_bytes=48 * 1024 * 1024
+        ),
+    )(*sums)
+    return (result[:4], result[4:])
+
+
+def small_sizes(width, hidden):
+    return (width, width, 2 * width, width, width, width, hidden, width)
+
+
+def finish_kernel(*refs):
+    ins, outs = (refs[:5], refs[5:])
+    for src, dst in zip(ins[:4], outs[:4]):
+        dst[...] = src[...].astype(jnp.float32)
+
+    @pl.when(pl.program_id(0) == 0)
+    def _():
+        small, line = (ins[4], 0)
+        for dst in outs[4:]:
+            for i in range(dst.shape[1] // COLS):
+                piece, row = divmod(line, small.shape[1])
+                dst[:, i * COLS : (i + 1) * COLS] = small[piece, row : row + 1, :].astype(
+                    jnp.float32
+                )
+                line += 1
 
 
 def sum_weight_grads_plain(lefts, rights, small, width):
@@ -764,7 +927,10 @@
     totals = lax.psum_scatter(totals, "dp", scatter_dimension=0, tiled=True)
     whole = lax.all_gather(as_sent(totals), "dp", axis=0, tiled=True)
     whole = jax.tree.map(lambda part: part.astype(jnp.float32), whole)
-    return whole[:4] + (whole[4][: small.size],)
+    sizes = small_sizes(width, hidden)
+    starts = [sum(sizes[:i]) for i in range(len(sizes))]
+    parts = [whole[4][None, s : s + size] for s, size in zip(starts, sizes)]
+    return (whole[:4], parts)
 
 
 def per_device(
@@ -803,35 +969,25 @@
             )
         )
     )
-    keeps = keep_masks[0, :, :, 0].astype(jnp.float32) * survive
+    keeps = keep_masks[0, :, :, 0]
     outputs, d_inputs, lefts, rights, small = run_layers(inputs, cotangent, weights, keeps)
-    layer_outputs = outputs[None, :, None]
-    input_grads = d_inputs[None, :, None]
-    width = inputs.shape[-1]
-    qkv, proj, up, down, small = sum_weight_grads(lefts, rights, small, width)
-    hidden = up.shape[1]
-    sizes = (width, width, 2 * width, width, width, width, hidden, width)
-    starts = [sum(sizes[:i]) for i in range(len(sizes))]
-    parts = [small[s : s + size] for s, size in zip(starts, sizes)]
-    whole = (
-        parts[0], parts[1], qkv, parts[2], proj, parts[3],
-        parts[4], parts[5], up, parts[6], down, parts[7],
-    )
+    big, small = sum_weight_grads(lefts, rights, small, inputs.shape[-1])
+    qkv, proj, up, down = (x[None] for x in big)
     return (
-        layer_outputs,
-        input_grads,
-        whole[0][None],
-        whole[1][None],
-        whole[2][None],
-        whole[3][None],
-        whole[4][None],
-        whole[5][None],
-        whole[6][None],
-        whole[7][None],
-        whole[8][None],
-        whole[9][None],
-        whole[10][None],
-        whole[11][None],
+        outputs[None, :, None],
+        d_inputs[None, :, None],
+        small[0],
+        small[1],
+        qkv,
+        small[2],
+        proj,
+        small[3],
+        small[4],
+        small[5],
+        up,
+        small[6],
+        down,
+        small[7],
     )
 
 

time: 381 us -> 298 us (0.78)
  Pallas kernels: 344 us -> 282 us
  other arithmetic: 18.9 us -> 0 us
    pallas_call x1, Pallas kernels: 229 us -> 157 us  [sum_weight_grads(): pl.pallas_call(functools.partial(reduce_kernel, count, width, hidden), ou...]
    another operation x4 -> x0, other arithmetic: 16.5 us -> none  [the longest x1 5.05 us: per_device(): whole[8][None]]
    pallas_call x0 -> x1, Pallas kernels: none -> 13.2 us  [sum_weight_grads(): pl.pallas_call(finish_kernel, grid=(steps,), out_shape=[jax.ShapeDtypeStr...]
    pallas_call x1, Pallas kernels: 43.4 us -> 39.6 us  [run_layers(): pl.pallas_call(forward_kernel, grid=(micro,), out_shape=(jax.ShapeDtypeSt...]
    unnamed x23 -> x10, local copies, waits for them, and re-layouts: 15.6 us -> 14.7 us
where the time goes in v3:
time: 298 us; the launch traced here: 297 us
  Pallas kernels  282 us (95%)
  local copies, waits for them, and re-layouts  14.7 us (5%)
    pallas_call x1, Pallas kernels, sum_weight_grads(): pl.pallas_call(functools.partial(reduce_kernel, count, width, hidden), ou...  157 us
    pallas_call x1, Pallas kernels, run_layers(): pl.pallas_call(backward_kernel, grid=(micro,), out_shape=(jax.ShapeDtypeS...  72.1 us
    pallas_call x1, Pallas kernels, run_layers(): pl.pallas_call(forward_kernel, grid=(micro,), out_shape=(jax.ShapeDtypeSt...  39.6 us
    unnamed x10, local copies, waits for them, and re-layouts  14.7 us
    pallas_call x1, Pallas kernels, sum_weight_grads(): pl.pallas_call(finish_kernel, grid=(steps,), out_shape=[jax.ShapeDtypeStr...  13.2 us

profile of v3, /device:TPU:1, one launch (start us, length us, event | category | flops | bytes accessed | tf_op | source)
XLA Modules:
  0.0 297.1 jit_solution(4985303440562506830)
XLA Ops:
  0.6 2.4 copy.29.in_ref
  3.1 2.4 copy.30.cot_ref
  5.5 39.6 %shard_map.254 = (bf16[4,198,768]{2,1,0:T(8,128)(2,1)}, bf16[4,208,768]{2,1,0:T(8,128)(2,1)}, bf16[4,208,5376]{2,1,0:T(8,128)(2,1)}, bf16[4,208,2304]{2,1,0:T(8,...) custom-call(s32[2,4]{1,0:T(2,128)} %bitcast.35, bf16[4,1,198,768]{3,2,1,0:T(8,128)(2,1)} %copy.29.in_ref, ...), custom_call_target="tpu_custom_call" | custom-call | tf_op jit(solution)/shard_map/pallas_call | solution.py:413
  45.1 2.8 copy.31
  47.9 72.1 %shard_map.255 = (bf16[4,198,768]{2,1,0:T(8,128)(2,1)}, bf16[4,208,6912]{2,1,0:T(8,128)(2,1)}, f32[48,256]{1,0:T(8,128)}) custom-call(s32[2,4]{1,0:T(2,128)} %bitcast.36, bf16[4,1,198,768]{3,2,1,0:T(8,128)(2,1)} %copy.30.cot_ref, bf16[4,208,768]{2,1,0:T(8,128)(2,1)} %get-tuple-element.41.held_ref, bf16[4,208,2304]{2,1,0:T(8,128)(2,1)} %get-tuple-element.42.qkv_ref, ...), custom_call_target="tpu_custom_call" | custom-call | tf_op jit(solution)/shard_map/pallas_call | solution.py:445
  119.9 2.8 copy.32
  122.7 156.7 %shard_map.256 = (bf16[16,48,2304]{2,1,0:T(8,128)(2,1)}, bf16[16,48,768]{2,1,0:T(8,128)(2,1)}, bf16[16,48,3072]{2,1,0:T(8,128)(2,1)}, bf16[4,16,48,768]{3,2,1,0:T(8,128)(2,1)}, bf16[16,48,256]{2,1,0:T(8,128)(2,1)}) custom-call(bf16[832,5376]{1,0:T(8,128)(2,1)} %bitcast.27, bf16[832,6912]{1,0:T(8,128)(2,1)} %bitcast.26, f32[1,48,256]{2,1,0:T(8,128)} %bitcast.34), custom_call_target="tpu_custom_call" | custom-call | tf_op jit(solution)/shard_map/pallas_call | solution.py:826
  279.5 0.0 copy-start
  279.5 2.0 copy-done
  281.5 0.0 copy-start.1
  281.5 1.3 copy-done.1
  282.7 0.0 copy-start.2
  282.7 1.0 copy-done.2
  283.7 13.2 %shard_map.257 = (f32[768,2304]{1,0:T(8,128)}, f32[768,768]{1,0:T(8,128)}, f32[768,3072]{1,0:T(8,128)}, f32[3072,768]{1,0:T(8,128)}, f32[1,768]{1,0:T(1,128)}, /...) custom-call(bf16[768,2304]{1,0:T(8,128)(2,1)S(1)} %bitcast.18, ...), custom_call_target="tpu_custom_call" | custom-call | tf_op jit(solution)/shard_map/pallas_call | solution.py:873
Async XLA Ops:
  279.5 2.0 copy-start
  281.5 1.3 copy-start.1
  282.7 1.0 copy-start.2
